TPU v7x, 512 devices: a whole 4x8x8 slice. The times are simulated.
512 devices in a mesh: tm: 128 (over z, y, core), space: 4 (over x).
Axes of the slice: x: 4, y: 8, z: 8, core: 2. Of those that a mesh axis runs over, the one named last changes fastest.
Arguments:
- right_side: float32 [512, 32, 256], P('tm', 'space'), may hold values from -24 to 24
- diffusion: float32 [32, 256], P('space'), may hold values from 0.5 to 4
- velocity: float32 [2, 32, 256], P(None, 'space'), may hold values from -0.5 to 0.5
Outputs:
- solution: float32 [512, 32, 256], P('tm', 'space')
- residual: float32 [512, 32, 256], P('tm', 'space')
All inputs are finite; a program needn't handle non-finite values.
Results may differ from a plain program's by a relative error of at most 0.0003.
Values sent between devices are 32-bit elements; how exact they have to be, the bound alone decides.
A program may use at most 64 MiB of HBM per device.

v0:
```python
import math

import jax
import jax.numpy as jnp
from jax import lax
from jax.sharding import Mesh
from jax.sharding import PartitionSpec as P

L = 512
KRYLOV = 3
SWEEPS = 3
TM = ("tm_0", "tm_1", "tm_2")
TM_SPACE = ("tm_0", "tm_1", "tm_2", "space")


alpha_corner = 0.05
damping = 0.8
epsilon = 1e-06
highest = lax.Precision.HIGHEST


def extended(block, sides, width):
    for axis, dim in sides:
        count = lax.axis_size(axis)
        forward = [(i, i + 1) for i in range(count - 1)]
        backward = [(target, source) for source, target in forward]
        low = lax.ppermute(
            lax.slice_in_dim(block, block.shape[dim] - width, None, axis=dim), axis, forward
        )
        high = lax.ppermute(lax.slice_in_dim(block, 0, width, axis=dim), axis, backward)
        block = jnp.concatenate([low, block, high], axis=dim)
    return block


def from_behind(block, axis, distance):
    devices = range(lax.axis_size(axis))
    route = [(i - distance, i) for i in devices if i - distance in devices]
    return lax.ppermute(block, axis, route)


def extended_2(value, sides, width):
    edges = {}
    for axis, dim in sides:
        size, length = (lax.axis_size(axis), value.shape[dim])
        up = [(i, (i + 1) % size) for i in range(size - 1)]
        last = lax.slice_in_dim(value, length - width, length, axis=dim)
        first = lax.slice_in_dim(value, 0, width, axis=dim)
        edges[dim] = (
            lax.ppermute(last, axis, up),
            lax.ppermute(first, axis, [(b, a) for a, b in up]),
        )
    done = []
    for _, dim in sides:
        low, high = edges[dim]
        around = [(width, width) if d in done else (0, 0) for d in range(value.ndim)]
        value = jnp.concatenate([jnp.pad(low, around), value, jnp.pad(high, around)], axis=dim)
        done.append(dim)
    return value


def cut_along(value, dim, length):
    shape = value.shape
    blocks = value.reshape(*shape[:dim], length, shape[dim] // length, *shape[dim + 1 :])
    return jnp.moveaxis(blocks, dim, 0)


def in_order(blocks, dim):
    shape = list(blocks.shape[1:])
    shape[dim] *= blocks.shape[0]
    return jnp.moveaxis(blocks, 0, dim).reshape(shape)


def turned_blocks(blocks, axes, turns):
    inside = blocks.shape[1:]
    out = blocks.reshape(*(lax.axis_size(a) for a in axes), *inside)
    for k in turns:
        out = lax.all_to_all(out, axes[k], k, k, tiled=True)
    return out.reshape(-1, *inside)


def core_and_chips(value, groups, turns, split_dim, concat_dim):
    length = lax.axis_size(groups[0]) * lax.axis_size(groups[1])
    blocks = cut_along(value, split_dim, length)
    return in_order(turned_blocks(blocks, groups, turns), concat_dim)


def one_axis_at_a_time(value, axes):
    for axis in axes:
        value = lax.psum(value, axis)
    return value


def shifted(padded, row_dim, col_dim, rows, cols, row_start, col_start):
    piece = lax.slice_in_dim(padded, row_start, row_start + rows, axis=row_dim)
    return lax.slice_in_dim(piece, col_start, col_start + cols, axis=col_dim)


def stencil(field, padded, row_dim, col_dim, diffusion, velocity_col, velocity_row):
    rows = field.shape[row_dim]
    cols = field.shape[col_dim]
    north = shifted(padded, row_dim, col_dim, rows, cols, 0, 1)
    south = shifted(padded, row_dim, col_dim, rows, cols, 2, 1)
    west = shifted(padded, row_dim, col_dim, rows, cols, 1, 0)
    east = shifted(padded, row_dim, col_dim, rows, cols, 1, 2)
    return (
        (1.0 + 4.0 * diffusion) * field
        - diffusion * (north + south + west + east)
        + velocity_col * (east - west)
        + velocity_row * (south - north)
    )


def divided(real_part, imag_part, diag_real, diag_imag, modulus):
    return (
        damping * (real_part * diag_real + imag_part * diag_imag) / modulus,
        damping * (imag_part * diag_real - real_part * diag_imag) / modulus,
    )


def remainder(
    source_real, source_imag, image_real, image_imag, guess_real, guess_imag, shift_real, shift_imag
):
    return (
        source_real - (image_real - (shift_real * guess_real + shift_imag * guess_imag)),
        source_imag - (image_imag - (shift_real * guess_imag - shift_imag * guess_real)),
    )


def dft_tables(length):
    index = jnp.arange(length, dtype=jnp.int32)
    product = index[:, None] * index[None, :] % length
    angle = product.astype(jnp.float32) * (2.0 * math.pi / length)
    return (jnp.cos(angle), jnp.sin(angle))


def least_squares(hessen, beta):
    ortho = []
    upper = [[None] * KRYLOV for row in range(KRYLOV)]
    for column in range(KRYLOV):
        current = hessen[:, column]
        for row in range(column):
            factor = jnp.sum(ortho[row] * current)
            upper[row][column] = factor
            current = current - factor * ortho[row]
        length = jnp.sqrt(jnp.sum(current * current))
        upper[column][column] = length
        ortho.append(current / length)
    target = [ortho[row][0] * beta for row in range(KRYLOV)]
    values = [None] * KRYLOV
    for row in reversed(range(KRYLOV)):
        accum = target[row]
        for later in range(row + 1, KRYLOV):
            accum = accum - upper[row][later] * values[later]
        values[row] = accum / upper[row][row]
    return jnp.stack(values)


def per_device(right_side, diffusion, velocity):
    steps_here = right_side.shape[0]
    devices_tm = lax.axis_size(TM)
    position = lax.axis_index(TM)
    log_decay = math.log(alpha_corner) / L
    decay = math.exp(log_decay)
    local_steps = position * steps_here + jnp.arange(steps_here, dtype=jnp.int32)
    times = local_steps.astype(jnp.float32)
    weights = jnp.exp(times * log_decay)[:, None, None]
    unweights = jnp.exp(-times * log_decay)[:, None, None]
    cosine, sine = dft_tables(L)
    velocity_col = velocity[0]
    velocity_row = velocity[1]
    width = right_side.shape[2] // devices_tm
    start = position * width
    diff_strip = lax.dynamic_slice_in_dim(diffusion, start, width, 1)[:, :, None]
    col_strip = lax.dynamic_slice_in_dim(velocity_col, start, width, 1)[:, :, None]
    row_strip = lax.dynamic_slice_in_dim(velocity_row, start, width, 1)[:, :, None]
    angles = jnp.arange(L, dtype=jnp.int32).astype(jnp.float32) * (2.0 * math.pi / L)
    shift_real = decay * jnp.cos(angles)
    shift_imag = decay * jnp.sin(angles)
    diag_real = 1.0 + 4.0 * diff_strip - shift_real
    modulus = diag_real * diag_real + shift_imag * shift_imag

    def forward(block):
        real_part = jnp.dot(block, cosine, precision=highest)
        imag_part = -jnp.dot(block, sine, precision=highest)
        return jnp.concatenate([real_part, imag_part], axis=2)

    total = one_axis_at_a_time(jnp.sum(right_side * right_side), TM_SPACE)
    beta = jnp.sqrt(total + epsilon)
    basis = [right_side / beta]
    prepared = []
    hessen = jnp.zeros((KRYLOV + 1, KRYLOV), jnp.float32)
    for column in range(KRYLOV):
        moved = jnp.transpose(basis[column] * weights, (1, 2, 0))
        spectrum = forward(lax.all_to_all(moved, TM, split_axis=1, concat_axis=2, tiled=True))
        source_real = spectrum[:, :, :L]
        source_imag = spectrum[:, :, L:]
        guess_real, guess_imag = divided(source_real, source_imag, diag_real, shift_imag, modulus)
        for sweep in range(SWEEPS - 1):
            joined = jnp.concatenate([guess_real, guess_imag], axis=2)
            padded = extended_2(joined, ((TM, 1), ("space", 0)), 1)
            image = stencil(joined, padded, 0, 1, diff_strip, col_strip, row_strip)
            left_real, left_imag = remainder(
                source_real,
                source_imag,
                image[:, :, :L],
                image[:, :, L:],
                guess_real,
                guess_imag,
                shift_real,
                shift_imag,
            )
            step_real, step_imag = divided(left_real, left_imag, diag_real, shift_imag, modulus)
            guess_real = guess_real + step_real
            guess_imag = guess_imag + step_imag
        back = (
            jnp.dot(guess_real, cosine, precision=highest)
            - jnp.dot(guess_imag, sine, precision=highest)
        ) / L
        back = core_and_chips(back, (("tm_0", "tm_1"), "tm_2"), (1, 0), 2, 1)
        direction = jnp.transpose(back, (2, 0, 1)) * unweights
        prepared.append(direction)
        apply_padded = extended(direction, (("space", 1),), 1)
        apply_padded = jnp.pad(apply_padded, ((0, 0), (0, 0), (1, 1)))
        apply_image = stencil(direction, apply_padded, 1, 2, diffusion, velocity_col, velocity_row)
        earlier = from_behind(direction[-1:], TM, 1)
        image = apply_image - jnp.concatenate([earlier, direction[:-1]], axis=0)
        local = jnp.stack([jnp.sum(vector * image) for vector in basis])
        projections, whole = (
            one_axis_at_a_time(local, TM_SPACE),
            one_axis_at_a_time(jnp.sum(image * image), TM_SPACE),
        )
        for row in range(column + 1):
            image = image - projections[row] * basis[row]
        squares = whole - jnp.sum(projections * projections)
        length = jnp.sqrt(squares + epsilon)
        hessen = hessen.at[: column + 1, column].set(projections)
        hessen = hessen.at[column + 1, column].set(length)
        basis.append(image / length)
    coeffs = least_squares(hessen, beta)
    solution = prepared[0] * coeffs[0]
    for column in range(1, KRYLOV):
        solution = solution + prepared[column] * coeffs[column]
    first = (jnp.arange(KRYLOV + 1) == 0).astype(jnp.float32)
    target = beta * first - jnp.sum(hessen * coeffs[None, :], axis=1)
    residual = basis[0] * target[0]
    for row in range(1, KRYLOV + 1):
        residual = residual + basis[row] * target[row]
    return (solution, residual)


def solution(mesh):
    torus = Mesh(
        mesh.devices.reshape(8, 8, 2, mesh.shape["space"]), ("tm_0", "tm_1", "tm_2", "space")
    )
    placed = (P(TM, "space", None), P("space", None), P(None, "space", None))
    return jax.shard_map(
        per_device,
        mesh=torus,
        in_specs=placed,
        out_specs=(P(TM, "space", None), P(TM, "space", None)),
        check_vma=False,
    )
```

profile of v0, /device:TPU:1, one launch (start us, length us, event | category | flops | bytes accessed | tf_op | source)
XLA Modules:
  0.0 585.0 jit_solution(895958468352536674)
XLA Ops:
  2.1 20.9 %psum.196 = f32[]{:T(128)} all-reduce(f32[]{:T(128)} %multiply_reduce_fusion.9), channel_id=1, replica_groups=mesh['tm_0'=8,'tm_1'=8,'tm_2'=2,'space'=4] {'tm_0'}, use_global_device_ids=true, to_apply=%region_1.2 | all-reduce | flops 1 | bytes 8 | tf_op jit(solution)/shard_map/psum | solution.py:89
  22.9 14.5 %psum.197 = f32[]{:T(128)} all-reduce(f32[]{:T(128)} %psum.196), channel_id=1, replica_groups=mesh['tm_0'=8,'tm_1'=8,'tm_2'=2,'space'=4] {'tm_1'}, use_global_device_ids=true, to_apply=%region_2.3 | all-reduce | flops 1 | bytes 8 | tf_op jit(solution)/shard_map/psum | solution.py:89
  37.4 10.9 %psum.198 = f32[]{:T(128)} all-reduce(f32[]{:T(128)} %psum.197), channel_id=1, replica_groups=mesh['tm_0'=8,'tm_1'=8,'tm_2'=2,'space'=4] {'tm_2'}, use_global_device_ids=true, to_apply=%region_3.4 | all-reduce | flops 1 | bytes 8 | tf_op jit(solution)/shard_map/psum | solution.py:89
  48.4 9.1 %psum.199 = f32[]{:T(128)} all-reduce(f32[]{:T(128)} %psum.198), channel_id=1, replica_groups=mesh['tm_0'=8,'tm_1'=8,'tm_2'=2,'space'=4] {'space'}, use_global_device_ids=true, to_apply=%region_4.5 | all-reduce | flops 1 | bytes 8 | tf_op jit(solution)/shard_map/psum | solution.py:89
  59.2 8.9 %all-to-all-start = ((f32[8,256,4]{0,2,1:T(4,128)}), f32[8,256,4]{0,2,1:T(4,128)S(1)}, u32[]{:S(2)}, u32[]{:S(2)}) async-start(f32[8,256,4]{0,2,1:T(4,128)} %copy.241), calls=%async_computation | async-start | bytes 1048576 | tf_op jit(solution)/shard_map/all_to_all | solution.py:194
  69.0 19.6 %all-to-all-done = f32[8,256,4]{0,2,1:T(4,128)S(1)} async-done(((f32[8,256,4]{0,2,1:T(4,128)}), f32[8,256,4]{0,2,1:T(4,128)S(1)}, u32[]{:S(2)}, u32[]{:S(2)}) %all-to-all-start) | async-done | bytes 32800 | tf_op jit(solution)/shard_map/all_to_all | solution.py:194
  89.1 5.3 convolution_negate_fusion.2
  94.4 5.3 fusion.92
  102.3 3.4 collective-permute-start.1
  108.0 3.0 collective-permute-done.2
  113.1 2.4 collective-permute-start.6
  115.5 4.3 collective-permute-start.4
  121.6 2.6 collective-permute-done.7
  124.3 4.6 fusion.20
  128.9 4.6 fusion.2
  134.2 4.2 all_to_all.84
  141.2 11.1 %all-to-all-start.2 = ((f32[64,1,128]{2,1,0:T(1,128)}), f32[64,1,128]{2,1,0:T(1,128)S(1)}, u32[]{:S(2)}, u32[]{:S(2)}) async-start(f32[64,1,128]{2,1,0:T(1,128)} %reshape.295), calls=%async_computation.2 | async-start | bytes 65536 | tf_op jit(solution)/shard_map/all_to_all | solution.py:77
  152.3 10.8 %all-to-all-done.2 = f32[64,1,128]{2,1,0:T(1,128)S(1)} async-done(((f32[64,1,128]{2,1,0:T(1,128)}), f32[64,1,128]{2,1,0:T(1,128)S(1)}, u32[]{:S(2)}, u32[]{:S(2)}) %all-to-all-start.2) | async-done | bytes 32800 | tf_op jit(solution)/shard_map/all_to_all | solution.py:77
  165.5 2.8 collective-permute-start.8
  169.6 4.2 collective-permute-start.10
  175.3 12.0 %all-reduce.21 = (f32[]{:T(128)}, f32[1]{0:T(128)}) all-reduce(f32[]{:T(128)} %get-tuple-element.90, f32[1]{0:T(128)} %bitcast.17), channel_id=1, replica_groups=mesh['tm_0'=8,'tm_1'=8,'tm_2'=2,'space'=4] {'tm_0'}, use_global_device_ids=true, to_apply=%region_11.12 | all-reduce | flops 2 | bytes 16 | tf_op jit(solution)/shard_map/psum | solution.py:89
  187.3 13.5 %all-reduce.18 = (f32[]{:T(128)}, f32[1]{0:T(128)}) all-reduce(f32[]{:T(128)} %get-tuple-element.103, f32[1]{0:T(128)} %get-tuple-element.104), channel_id=1, replica_groups=mesh['tm_0'=8,'tm_1'=8,'tm_2'=2,'space'=4] {'tm_1'}, use_global_device_ids=true, to_apply=%region_12.13 | all-reduce | flops 2 | bytes 16 | tf_op jit(solution)/shard_map/psum | solution.py:89
  200.7 11.8 %all-reduce.27 = (f32[]{:T(128)}, f32[1]{0:T(128)}) all-reduce(f32[]{:T(128)} %get-tuple-element.97, f32[1]{0:T(128)} %get-tuple-element.98), channel_id=1, replica_groups=mesh['tm_0'=8,'tm_1'=8,'tm_2'=2,'space'=4] {'tm_2'}, use_global_device_ids=true, to_apply=%region_13.14 | all-reduce | flops 2 | bytes 16 | tf_op jit(solution)/shard_map/psum | solution.py:89
  212.5 9.0 %all-reduce.24 = (f32[]{:T(128)}, f32[1]{0:T(128)}) all-reduce(f32[]{:T(128)} %get-tuple-element.115, f32[1]{0:T(128)} %get-tuple-element.116), channel_id=1, replica_groups=mesh['tm_0'=8,'tm_1'=8,'tm_2'=2,'space'=4] {'space'}, use_global_device_ids=true, to_apply=%region_14.15 | all-reduce | flops 2 | bytes 16 | tf_op jit(solution)/shard_map/psum | solution.py:89
  224.6 29.7 %all_to_all.85 = f32[8,256,4]{0,2,1:T(4,128)S(1)} all-to-all(f32[8,256,4]{0,2,1:T(4,128)S(1)} %copy.257), channel_id=1, replica_groups=mesh['tm_0'=8,'tm_1'=8,'tm_2'=2,'space'=4] {'tm_0','tm_1','tm_2'}, dimensions={1} | all-to-all | bytes 65536 | tf_op jit(solution)/shard_map/all_to_all | solution.py:194
  254.7 5.3 convolution_negate_fusion.1
  260.0 5.3 fusion.105
  265.3 3.2 collective-permute-start.12
  273.1 3.1 collective-permute-done.14
  276.5 5.1 collective-permute-start.16
  283.5 2.7 collective-permute-start.15
  287.5 3.1 collective-permute-done.18
  290.7 4.6 fusion.16
  295.3 4.7 fusion.1
  300.5 3.6 all_to_all.86
  305.9 23.0 %all_to_all.87 = f32[64,1,128]{2,1,0:T(1,128)S(1)} all-to-all(f32[64,1,128]{2,1,0:T(1,128)S(1)} %reshape.299), channel_id=1, replica_groups=mesh['tm_0'=8,'tm_1'=8,'tm_2'=2,'space'=4] {'tm_0','tm_1'}, dimensions={0} | all-to-all | bytes 65536 | tf_op jit(solution)/shard_map/all_to_all | solution.py:77
  334.6 4.2 collective-permute-start.21
  341.6 11.9 %all-reduce.20 = (f32[]{:T(128)}, f32[2]{0:T(128)S(1)}) all-reduce(f32[]{:T(128)} %get-tuple-element.87, f32[2]{0:T(128)S(1)} %pad_maximum_fusion.72), channel_id=1, replica_groups=mesh['tm_0'=8,'tm_1'=8,'tm_2'=2,'space'=4] {'tm_0'}, use_global_device_ids=true, to_apply=%region_23.24 | all-reduce | flops 3 | bytes 24 | tf_op jit(solution)/shard_map/psum | solution.py:89
  353.5 13.5 %all-reduce.17 = (f32[]{:T(128)}, f32[2]{0:T(128)S(1)}) all-reduce(f32[]{:T(128)} %get-tuple-element.101, f32[2]{0:T(128)S(1)} %get-tuple-element.102), channel_id=1, replica_groups=mesh['tm_0'=8,'tm_1'=8,'tm_2'=2,'space'=4] {'tm_1'}, use_global_device_ids=true, to_apply=%region_24.25 | all-reduce | flops 3 | bytes 24 | tf_op jit(solution)/shard_map/psum | solution.py:89
  367.0 11.7 %all-reduce.26 = (f32[]{:T(128)}, f32[2]{0:T(128)S(1)}) all-reduce(f32[]{:T(128)} %get-tuple-element.95, f32[2]{0:T(128)S(1)} %get-tuple-element.96), channel_id=1, replica_groups=mesh['tm_0'=8,'tm_1'=8,'tm_2'=2,'space'=4] {'tm_2'}, use_global_device_ids=true, to_apply=%region_25.26 | all-reduce | flops 3 | bytes 24 | tf_op jit(solution)/shard_map/psum | solution.py:89
  378.7 9.0 %all-reduce.23 = (f32[]{:T(128)}, f32[2]{0:T(128)S(1)}) all-reduce(f32[]{:T(128)} %get-tuple-element.113, f32[2]{0:T(128)S(1)} %get-tuple-element.114), channel_id=1, replica_groups=mesh['tm_0'=8,'tm_1'=8,'tm_2'=2,'space'=4] {'space'}, use_global_device_ids=true, to_apply=%region_26.27 | all-reduce | flops 3 | bytes 24 | tf_op jit(solution)/shard_map/psum | solution.py:89
  392.5 9.4 %all-to-all-start.6 = ((f32[8,256,4]{0,2,1:T(4,128)}), f32[8,256,4]{0,2,1:T(4,128)S(1)}, u32[]{:S(2)}, u32[]{:S(2)}) async-start(f32[8,256,4]{0,2,1:T(4,128)} %copy.268), calls=%async_computation.6 | async-start | bytes 1048576 | tf_op jit(solution)/shard_map/all_to_all | solution.py:194
  402.6 19.8 %all-to-all-done.6 = f32[8,256,4]{0,2,1:T(4,128)S(1)} async-done(((f32[8,256,4]{0,2,1:T(4,128)}), f32[8,256,4]{0,2,1:T(4,128)S(1)}, u32[]{:S(2)}, u32[]{:S(2)}) %all-to-all-start.6) | async-done | bytes 32800 | tf_op jit(solution)/shard_map/all_to_all | solution.py:194
  422.9 5.3 convolution_negate_fusion
  428.2 5.3 fusion.99
  436.1 3.2 collective-permute-start.23
  441.9 2.6 collective-permute-done.24
  444.8 4.3 collective-permute-start.26
  450.6 2.2 collective-permute-start.27
  452.8 2.1 collective-permute-start.28
  455.7 2.4 collective-permute-done.28
  458.2 4.6 fusion.12
  462.8 4.6 fusion
  468.0 3.4 all_to_all.88
  473.7 11.5 %all-to-all-start.8 = ((f32[64,1,128]{2,1,0:T(1,128)}), f32[64,1,128]{2,1,0:T(1,128)S(1)}, u32[]{:S(2)}, u32[]{:S(2)}) async-start(f32[64,1,128]{2,1,0:T(1,128)} %reshape.303), calls=%async_computation.8 | async-start | bytes 65536 | tf_op jit(solution)/shard_map/all_to_all | solution.py:77
  486.6 9.4 %all-to-all-done.8 = f32[64,1,128]{2,1,0:T(1,128)S(1)} async-done(((f32[64,1,128]{2,1,0:T(1,128)}), f32[64,1,128]{2,1,0:T(1,128)S(1)}, u32[]{:S(2)}, u32[]{:S(2)}) %all-to-all-start.8) | async-done | bytes 32800 | tf_op jit(solution)/shard_map/all_to_all | solution.py:77
  498.4 4.3 collective-permute-start.30
  507.6 4.2 collective-permute-start.32
  513.3 2.0 pad_maximum_fusion.73
  515.3 11.9 %all-reduce.19 = (f32[3]{0:T(128)S(1)}, f32[]{:T(128)}) all-reduce(f32[3]{0:T(128)S(1)} %pad_maximum_fusion.73, f32[]{:T(128)} %get-tuple-element.82), channel_id=1, replica_groups=mesh['tm_0'=8,'tm_1'=8,'tm_2'=2,'space'=4] {'tm_0'}, use_global_device_ids=true, to_apply=%region_32.33 | all-reduce | flops 4 | bytes 32 | tf_op jit(solution)/shard_map/psum | solution.py:89
  527.3 13.5 %all-reduce.16 = (f32[3]{0:T(128)S(1)}, f32[]{:T(128)}) all-reduce(f32[3]{0:T(128)S(1)} %get-tuple-element.99, f32[]{:T(128)} %get-tuple-element.100), channel_id=1, replica_groups=mesh['tm_0'=8,'tm_1'=8,'tm_2'=2,'space'=4] {'tm_1'}, use_global_device_ids=true, to_apply=%region_33.34 | all-reduce | flops 4 | bytes 32 | tf_op jit(solution)/shard_map/psum | solution.py:89
  540.7 11.7 %all-reduce.25 = (f32[3]{0:T(128)S(1)}, f32[]{:T(128)}) all-reduce(f32[3]{0:T(128)S(1)} %get-tuple-element.93, f32[]{:T(128)} %get-tuple-element.94), channel_id=1, replica_groups=mesh['tm_0'=8,'tm_1'=8,'tm_2'=2,'space'=4] {'tm_2'}, use_global_device_ids=true, to_apply=%region_34.35 | all-reduce | flops 4 | bytes 32 | tf_op jit(solution)/shard_map/psum | solution.py:89
  552.4 9.3 %all-reduce.22 = (f32[3]{0:T(128)S(1)}, f32[]{:T(128)}) all-reduce(f32[3]{0:T(128)S(1)} %get-tuple-element.111, f32[]{:T(128)} %get-tuple-element.112), channel_id=1, replica_groups=mesh['tm_0'=8,'tm_1'=8,'tm_2'=2,'space'=4] {'space'}, use_global_device_ids=true, to_apply=%region_35.36 | all-reduce | flops 4 | bytes 32 | tf_op jit(solution)/shard_map/psum | solution.py:89
  579.6 4.9 multiply_add_fusion
  (184 shorter events, 79.0 us)
Async XLA Ops:
  0.6 57.5 %copy-start = (f32[4,8,256]{2,1,0:T(8,128)S(1)}, f32[4,8,256]{2,1,0:T(8,128)}, u32[]{:S(2)}) copy-start(f32[4,8,256]{2,1,0:T(8,128)} %param.15) | copy-start | bytes 98308
  59.2 29.5 %all-to-all-start = ((f32[8,256,4]{0,2,1:T(4,128)}), f32[8,256,4]{0,2,1:T(4,128)S(1)}, u32[]{:S(2)}, u32[]{:S(2)}) async-start(f32[8,256,4]{0,2,1:T(4,128)} %copy.241), calls=%async_computation | async-start | bytes 1048576 | tf_op jit(solution)/shard_map/all_to_all | solution.py:194
  68.1 0.7 copy-start.1
  68.1 0.8 copy-start.2
  99.7 8.3 %collective-permute-start = (f32[1,2,1024]{2,0,1:T(1,128)S(1)}, f32[1,2,1024]{2,0,1:T(1,128)S(1)}, u32[]{:S(2)}, u32[]{:S(2)}) collective-permute-start(f32[1,2,1024]{2,0,1:T(1,128)S(1)} %get-tuple-element.164), channel_id=1, source_target_pairs={{0,1},{1,2},{2,3},{4,5},{5,6},{6,7},{8,9},{9,10},{10,11},{12,13},{... | collective-permute-start | bytes 24584 | tf_op jit(solution)/shard_map/ppermute | solution.py:49
  101.0 7.0 %collective-permute-start.3 = (f32[1,2,1024]{2,0,1:T(1,128)S(1)}, f32[1,2,1024]{2,0,1:T(1,128)S(1)}, u32[]{:S(2)}, u32[]{:S(2)}) collective-permute-start(f32[1,2,1024]{2,0,1:T(1,128)S(1)} %get-tuple-element.163), channel_id=1, source_target_pairs={{1,0},{2,1},{3,2},{5,4},{6,5},{7,6},{9,8},{10,9},{11,10},{13,12},{... | collective-permute-start | bytes 24584 | tf_op jit(solution)/shard_map/ppermute | solution.py:50
  102.3 5.7 collective-permute-start.1
  105.7 5.2 collective-permute-start.2
  111.2 13.0 %collective-permute-start.5 = (f32[8,1,1024]{2,0,1:T(8,128)S(1)}, f32[8,1,1024]{2,0,1:T(8,128)S(1)}, u32[]{:S(2)}, u32[]{:S(2)}) collective-permute-start(f32[8,1,1024]{2,0,1:T(8,128)S(1)} %get-tuple-element.161), channel_id=1, source_target_pairs={{0,4},{4,8},{8,12},{12,16},{16,20},{20,24},{24,28},{28,32},{32,36}... | collective-permute-start | bytes 98312 | tf_op jit(solution)/shard_map/ppermute | solution.py:49
  113.1 11.1 %collective-permute-start.6 = (f32[8,1,1024]{2,0,1:T(8,128)S(1)}, f32[8,1,1024]{2,0,1:T(8,128)S(1)}, u32[]{:S(2)}, u32[]{:S(2)}) collective-permute-start(f32[8,1,1024]{2,0,1:T(8,128)S(1)} %get-tuple-element.162), channel_id=1, source_target_pairs={{4,0},{8,4},{12,8},{16,12},{20,16},{24,20},{28,24},{32,28},{36,32}... | collective-permute-start | bytes 98312 | tf_op jit(solution)/shard_map/ppermute | solution.py:50
  115.5 6.0 %collective-permute-start.4 = (f32[1,2,1024]{2,0,1:T(1,128)S(1)}, f32[1,2,1024]{2,0,1:T(1,128)S(1)}, u32[]{:S(2)}, u32[]{:S(2)}) collective-permute-start(f32[1,2,1024]{2,0,1:T(1,128)S(1)} %get-tuple-element.160), channel_id=1, source_target_pairs={{0,1},{1,2},{2,3},{4,5},{5,6},{6,7},{8,9},{9,10},{10,11},{12,13},{... | collective-permute-start | bytes 24584 | tf_op jit(solution)/shard_map/ppermute | solution.py:49
  119.8 4.4 collective-permute-start.7
  141.2 21.9 %all-to-all-start.2 = ((f32[64,1,128]{2,1,0:T(1,128)}), f32[64,1,128]{2,1,0:T(1,128)S(1)}, u32[]{:S(2)}, u32[]{:S(2)}) async-start(f32[64,1,128]{2,1,0:T(1,128)} %reshape.295), calls=%async_computation.2 | async-start | bytes 65536 | tf_op jit(solution)/shard_map/all_to_all | solution.py:77
  165.5 8.4 %collective-permute-start.8 = (f32[4,1,256]{2,1,0:T(1,128)S(1)}, f32[4,1,256]{2,1,0:T(1,128)S(1)}, u32[]{:S(2)}, u32[]{:S(2)}) collective-permute-start(f32[4,1,256]{2,1,0:T(1,128)S(1)} %get-tuple-element.171), channel_id=1, source_target_pairs={{0,1},{1,2},{2,3},{4,5},{5,6},{6,7},{8,9},{9,10},{10,11},{12,13},{... | collective-permute-start | bytes 12296 | tf_op jit(solution)/shard_map/ppermute | solution.py:27
  168.3 5.5 collective-permute-start.9
  169.6 5.0 collective-permute-start.10
  265.3 10.9 %collective-permute-start.12 = (f32[8,1,1024]{2,0,1:T(8,128)S(1)}, f32[8,1,1024]{2,0,1:T(8,128)S(1)}, u32[]{:S(2)}, u32[]{:S(2)}) collective-permute-start(f32[8,1,1024]{2,0,1:T(8,128)S(1)} %get-tuple-element.157), channel_id=1, source_target_pairs={{0,4},{4,8},{8,12},{12,16},{16,20},{20,24},{24,28},{28,32},{32,36}... | collective-permute-start | bytes 98312 | tf_op jit(solution)/shard_map/ppermute | solution.py:49
  268.5 7.7 %collective-permute-start.13 = (f32[8,1,1024]{2,0,1:T(8,128)S(1)}, f32[8,1,1024]{2,0,1:T(8,128)S(1)}, u32[]{:S(2)}, u32[]{:S(2)}) collective-permute-start(f32[8,1,1024]{2,0,1:T(8,128)S(1)} %get-tuple-element.158), channel_id=1, source_target_pairs={{4,0},{8,4},{12,8},{16,12},{20,16},{24,20},{28,24},{32,28},{36,32}... | collective-permute-start | bytes 98312 | tf_op jit(solution)/shard_map/ppermute | solution.py:50
  270.4 2.7 collective-permute-start.11
  271.8 4.4 collective-permute-start.14
  276.5 14.1 %collective-permute-start.16 = (f32[8,1,1024]{2,0,1:T(8,128)S(1)}, f32[8,1,1024]{2,0,1:T(8,128)S(1)}, u32[]{:S(2)}, u32[]{:S(2)}) collective-permute-start(f32[8,1,1024]{2,0,1:T(8,128)S(1)} %get-tuple-element.153), channel_id=1, source_target_pairs={{0,4},{4,8},{8,12},{12,16},{16,20},{20,24},{24,28},{28,32},{32,36}... | collective-permute-start | bytes 98312 | tf_op jit(solution)/shard_map/ppermute | solution.py:49
  281.5 9.1 %collective-permute-start.17 = (f32[8,1,1024]{2,0,1:T(8,128)S(1)}, f32[8,1,1024]{2,0,1:T(8,128)S(1)}, u32[]{:S(2)}, u32[]{:S(2)}) collective-permute-start(f32[8,1,1024]{2,0,1:T(8,128)S(1)} %get-tuple-element.154), channel_id=1, source_target_pairs={{4,0},{8,4},{12,8},{16,12},{20,16},{24,20},{28,24},{32,28},{36,32}... | collective-permute-start | bytes 98312 | tf_op jit(solution)/shard_map/ppermute | solution.py:50
  283.5 4.0 collective-permute-start.15
  286.2 4.4 collective-permute-start.18
  331.3 7.5 %collective-permute-start.19 = (f32[4,1,256]{2,1,0:T(1,128)S(1)}, f32[4,1,256]{2,1,0:T(1,128)S(1)}, u32[]{:S(2)}, u32[]{:S(2)}) collective-permute-start(f32[4,1,256]{2,1,0:T(1,128)S(1)} %get-tuple-element.169), channel_id=1, source_target_pairs={{0,1},{1,2},{2,3},{4,5},{5,6},{6,7},{8,9},{9,10},{10,11},{12,13},{... | collective-permute-start | bytes 12296 | tf_op jit(solution)/shard_map/ppermute | solution.py:27
  333.3 5.5 collective-permute-start.20
  334.6 5.0 collective-permute-start.21
  392.5 9.4 %copy-start.3 = (s32[2]{0:T(128)S(1)}, s32[2]{0:T(128)}, u32[]{:S(2)}) copy-start(s32[2]{0:T(128)} %constant.222.clone.1) | copy-start | bytes 28
  392.5 29.9 %all-to-all-start.6 = ((f32[8,256,4]{0,2,1:T(4,128)}), f32[8,256,4]{0,2,1:T(4,128)S(1)}, u32[]{:S(2)}, u32[]{:S(2)}) async-start(f32[8,256,4]{0,2,1:T(4,128)} %copy.268), calls=%async_computation.6 | async-start | bytes 1048576 | tf_op jit(solution)/shard_map/all_to_all | solution.py:194
  433.5 8.4 %collective-permute-start.22 = (f32[1,2,1024]{2,0,1:T(1,128)S(1)}, f32[1,2,1024]{2,0,1:T(1,128)S(1)}, u32[]{:S(2)}, u32[]{:S(2)}) collective-permute-start(f32[1,2,1024]{2,0,1:T(1,128)S(1)} %get-tuple-element.148), channel_id=1, source_target_pairs={{0,1},{1,2},{2,3},{4,5},{5,6},{6,7},{8,9},{9,10},{10,11},{12,13},{... | collective-permute-start | bytes 24584 | tf_op jit(solution)/shard_map/ppermute | solution.py:49
  434.8 7.1 %collective-permute-start.25 = (f32[1,2,1024]{2,0,1:T(1,128)S(1)}, f32[1,2,1024]{2,0,1:T(1,128)S(1)}, u32[]{:S(2)}, u32[]{:S(2)}) collective-permute-start(f32[1,2,1024]{2,0,1:T(1,128)S(1)} %get-tuple-element.147), channel_id=1, source_target_pairs={{1,0},{2,1},{3,2},{5,4},{6,5},{7,6},{9,8},{10,9},{11,10},{13,12},{... | collective-permute-start | bytes 24584 | tf_op jit(solution)/shard_map/ppermute | solution.py:50
  436.1 5.8 collective-permute-start.23
  439.3 5.2 collective-permute-start.24
  444.8 10.8 %collective-permute-start.26 = (f32[1,2,1024]{2,0,1:T(1,128)S(1)}, f32[1,2,1024]{2,0,1:T(1,128)S(1)}, u32[]{:S(2)}, u32[]{:S(2)}) collective-permute-start(f32[1,2,1024]{2,0,1:T(1,128)S(1)} %get-tuple-element.144), channel_id=1, source_target_pairs={{0,1},{1,2},{2,3},{4,5},{5,6},{6,7},{8,9},{9,10},{10,11},{12,13},{... | collective-permute-start | bytes 24584 | tf_op jit(solution)/shard_map/ppermute | solution.py:49
  449.1 6.6 %collective-permute-start.29 = (f32[1,2,1024]{2,0,1:T(1,128)S(1)}, f32[1,2,1024]{2,0,1:T(1,128)S(1)}, u32[]{:S(2)}, u32[]{:S(2)}) collective-permute-start(f32[1,2,1024]{2,0,1:T(1,128)S(1)} %get-tuple-element.143), channel_id=1, source_target_pairs={{1,0},{2,1},{3,2},{5,4},{6,5},{7,6},{9,8},{10,9},{11,10},{13,12},{... | collective-permute-start | bytes 24584 | tf_op jit(solution)/shard_map/ppermute | solution.py:50
  450.6 5.0 collective-permute-start.27
  452.8 5.2 collective-permute-start.28
  473.7 22.3 %all-to-all-start.8 = ((f32[64,1,128]{2,1,0:T(1,128)}), f32[64,1,128]{2,1,0:T(1,128)S(1)}, u32[]{:S(2)}, u32[]{:S(2)}) async-start(f32[64,1,128]{2,1,0:T(1,128)} %reshape.303), calls=%async_computation.8 | async-start | bytes 65536 | tf_op jit(solution)/shard_map/all_to_all | solution.py:77
  498.4 13.4 %collective-permute-start.30 = (f32[4,1,256]{2,1,0:T(1,128)S(1)}, f32[4,1,256]{2,1,0:T(1,128)S(1)}, u32[]{:S(2)}, u32[]{:S(2)}) collective-permute-start(f32[4,1,256]{2,1,0:T(1,128)S(1)} %get-tuple-element.167), channel_id=1, source_target_pairs={{0,1},{1,2},{2,3},{4,5},{5,6},{6,7},{8,9},{9,10},{10,11},{12,13},{... | collective-permute-start | bytes 12296 | tf_op jit(solution)/shard_map/ppermute | solution.py:27
  502.6 9.1 %collective-permute-start.31 = (f32[4,1,256]{2,1,0:T(1,128)S(1)}, f32[4,1,256]{2,1,0:T(1,128)S(1)}, u32[]{:S(2)}, u32[]{:S(2)}) collective-permute-start(f32[4,1,256]{2,1,0:T(1,128)S(1)} %get-tuple-element.168), channel_id=1, source_target_pairs={{1,0},{2,1},{3,2},{5,4},{6,5},{7,6},{9,8},{10,9},{11,10},{13,12},{... | collective-permute-start | bytes 12296 | tf_op jit(solution)/shard_map/ppermute | solution.py:30
  507.6 5.0 collective-permute-start.32
where the time goes:
time: 595 us; the launch traced here: 585 us
  blocking collectives  258 us (43%)
  starting transfers between devices  121 us (20%)
  waiting for transfers between devices  78.4 us (13%)
  matrix products  59.6 us (10%)
  other arithmetic  33.8 us (6%)
  local copies, waits for them, and re-layouts  22.3 us (4%)
  between operations  11.6 us (2%)
    psum x16, blocking collectives, one_axis_at_a_time(): value = lax.psum(value, axis)  194 us
    all_to_all x2, waiting for transfers between devices, per_device(): lax.all_to_all(moved, TM, split_axis=1, concat_axis=2, tiled=True)  39.5 us
    all_to_all x4, blocking collectives, turned_blocks(): out = lax.all_to_all(out, axes[k], k, k, tiled=True)  34.3 us
    ppermute x12, starting transfers between devices, extended_2(): lax.ppermute(last, axis, up)  34.1 us
    all_to_all x1, blocking collectives, per_device(): lax.all_to_all(moved, TM, split_axis=1, concat_axis=2, tiled=True)  29.7 us
    all_to_all x2, starting transfers between devices, turned_blocks(): out = lax.all_to_all(out, axes[k], k, k, tiled=True)  22.6 us
    ppermute x12, starting transfers between devices, extended_2(): lax.ppermute(first, axis, [(b, a) for a, b in up])  20.7 us
    all_to_all x2, waiting for transfers between devices, turned_blocks(): out = lax.all_to_all(out, axes[k], k, k, tiled=True)  20.2 us
  transfers between devices with their start and end apart: 37, of which 13 were waited for; matrix products, arithmetic and copies ran while one was open for 1% of the time, Pallas kernels for 0%

commit v1 on v0

v1 whole, which is shorter than its diff:
```python
import math

import jax
import jax.numpy as jnp
import numpy as np
from jax import lax
from jax.experimental import pallas as pl
from jax.experimental.pallas import tpu as pltpu
from jax.sharding import PartitionSpec as P

L = 512
KRYLOV = 3
ALPHA = 0.05
DAMPING = 0.8
EPSILON = 1e-06
LOG_DECAY = math.log(ALPHA) / L
DECAY = math.exp(LOG_DECAY)
MESH = pl.DeviceIdType.MESH
HIGHEST = lax.Precision.HIGHEST
F32 = jnp.float32


def tables():
    n = np.arange(L)
    k = np.arange(L // 2)
    angle = 2.0 * np.pi * ((n[:, None] * k[None, :]) % L) / L
    real = np.cos(angle)
    imag = -np.sin(angle)
    imag[:, 0] = np.where(n % 2 == 0, 1.0, -1.0)
    packed = np.concatenate([real, imag], axis=1)
    scale = np.full(L, 2.0 / L)
    scale[0] = scale[L // 2] = 1.0 / L
    decays = DECAY ** n
    forward = packed * decays[:, None]
    inverse = (packed * scale[None, :]).T / decays[None, :]
    shift_real = DECAY * np.cos(2.0 * np.pi * k / L)
    shift_imag = DECAY * np.sin(2.0 * np.pi * k / L)
    shift_other = shift_real.copy()
    shift_other[0] = -DECAY
    shift_imag[0] = 0.0
    corner = np.concatenate([shift_real * scale[: L // 2], shift_imag * scale[L // 2 :]])
    corner[L // 2] = -DECAY / L
    rows = np.concatenate([shift_real, shift_other, shift_imag, corner]).reshape(10, 128)
    small = np.zeros((16, 128))
    small[:10] = rows
    return forward.astype(np.float32), inverse.astype(np.float32), small.astype(np.float32)


def two_sum(a, b):
    s = a + b
    t = s - a
    return s, (a - (s - t)) + (b - t)


def split(a):
    c = 4097.0 * a
    high = c - (c - a)
    return high, a - high


def two_prod(a, b):
    p = a * b
    ah, al = split(a)
    bh, bl = split(b)
    return p, ((ah * bh - p) + ah * bl + al * bh) + al * bl


def pair_div(a, b):
    safe = jnp.where(b[0] > 0.0, b[0], 1.0)
    q = jnp.where(b[0] > 0.0, a[0] / safe, 0.0)
    p, e = two_prod(q, b[0])
    rest = ((a[0] - p) - e) + (a[1] - q * b[1])
    r = jnp.where(b[0] > 0.0, rest / safe, 0.0)
    s = q + r
    return s, r - (s - q)


def pair_less(a, m, b):
    p, e = two_prod(m[0], b[0])
    e = e + (m[0] * b[1] + m[1] * b[0])
    s, t = two_sum(a[0], -p)
    t = t + (a[1] - e)
    h = s + t
    return h, t - (h - s)


def krylov_weights(gram):
    n = KRYLOV + 1
    lower = [[None] * n for _ in range(n)]
    norm = [None] * n
    cross = [[None] * n for _ in range(n)]
    for k in range(n):
        for i in range(k, n):
            value = gram[k][i]
            for m in range(k):
                value = pair_less(value, lower[i][m], cross[k][m])
            cross[i][k] = value
        head = cross[k][k]
        keep = head[0] > 0.0
        head = (jnp.where(keep, head[0], 0.0), jnp.where(keep, head[1], 0.0))
        norm[k] = head[0]
        for i in range(k + 1, n):
            lower[i][k] = pair_div(cross[i][k], head)
    low = [[None if v is None else v[0] for v in row] for row in lower]
    zero = jnp.zeros_like(norm[0])
    images = []
    for k in range(KRYLOV):
        image = [low[k + 1][i] for i in range(k + 1)] + [zero + 1.0]
        for m in range(k):
            for i in range(m + 2):
                image[i] = image[i] - low[k][m] * images[m][i]
        images.append(image)
    beta = jnp.sqrt(norm[0] + EPSILON)
    basis = [[1.0 / beta]]
    hessen = [[zero] * KRYLOV for _ in range(n)]
    for j in range(KRYLOV):
        work = [zero] * (j + 2)
        for k in range(j + 1):
            for i in range(k + 2):
                work[i] = work[i] + basis[j][k] * images[k][i]
        for i in range(j + 1):
            total = zero
            for k in range(i + 1):
                total = total + basis[i][k] * norm[k] * work[k]
            hessen[i][j] = total
        for i in range(j + 1):
            for k in range(i + 1):
                work[k] = work[k] - hessen[i][j] * basis[i][k]
        total = zero
        for k in range(j + 2):
            total = total + work[k] * work[k] * norm[k]
        length = jnp.sqrt(total + EPSILON)
        hessen[j + 1][j] = length
        basis.append([v / length for v in work])
    ortho = []
    upper = [[None] * KRYLOV for _ in range(KRYLOV)]
    for column in range(KRYLOV):
        current = [hessen[i][column] for i in range(n)]
        for row in range(column):
            factor = sum(ortho[row][i] * current[i] for i in range(n))
            upper[row][column] = factor
            current = [current[i] - factor * ortho[row][i] for i in range(n)]
        length = jnp.sqrt(sum(v * v for v in current))
        upper[column][column] = length
        ortho.append([v / length for v in current])
    values = [None] * KRYLOV
    for row in reversed(range(KRYLOV)):
        accum = ortho[row][0] * beta
        for later in range(row + 1, KRYLOV):
            accum = accum - upper[row][later] * values[later]
        values[row] = accum / upper[row][row]
    target = []
    for i in range(n):
        accum = beta if i == 0 else zero
        for j in range(KRYLOV):
            accum = accum - hessen[i][j] * values[j]
        target.append(accum)

    def on_p(weights):
        on_u = [zero] * len(weights)
        for j, weight in enumerate(weights):
            for k in range(len(basis[j])):
                if k < len(weights):
                    on_u[k] = on_u[k] + weight * basis[j][k]
        for k in reversed(range(len(weights))):
            for i in range(k):
                on_u[i] = on_u[i] - low[k][i] * on_u[k]
        return on_u

    return on_p(values), on_p(target)


def lanes_below(count, shape=(8, 128)):
    return lax.broadcasted_iota(jnp.int32, shape, len(shape) - 1) < count


def lane_block(index):
    lane = lax.broadcasted_iota(jnp.int32, (8, 128), 1)
    return (lane >= 32 * index) & (lane < 32 * index + 32)


def turn(value, amount):
    amount = amount % 128
    return value if amount == 0 else pltpu.roll(value, amount, 1)


def kernel(
    b_ref, diff_ref, vel_ref, small_ref, fwd_hbm, inv_hbm,
    sol_ref, res_ref,
    fwd, inv,
    m1, r1, buf1, m2, r2, cd, cv, point, lead, own, edge4, edge2, h,
    left1, right1, left2, right2, north, south, nw, ne, sw, se, wa, wb,
    ar0, ar1, ar2, ars0, ars1, ars2, m3, r3, buf2, m4, r4,
    const_sem, coef_s, coef_r, s1_s, s1_r, s2_s, s2_r, ha_s, ha_r, a0_s, a0_r, a1_s, a1_r, a2_s, a2_r,
    s3_s, s3_r, s4_s, s4_r,
):
    tm = lax.axis_index("tm")
    x = lax.axis_index("space")
    z = tm // 16
    e_me = tm % 16
    y = e_me // 2
    core = e_me % 2
    odd = z % 2
    ys = y + odd * (7 - 2 * y)
    g = (z * 8 + ys) * 2 + core

    def at_strip(index):
        index = (index + 128) % 128
        strip = index // 2
        zz = strip // 8
        yy = strip % 8
        yy = yy + (zz % 2) * (7 - 2 * yy)
        return zz * 16 + yy * 2 + index % 2

    def place(t, s):
        return {"tm": t, "space": s}

    up = (x + 3) % 4
    down = (x + 1) % 4
    consts = [
        pltpu.make_async_copy(fwd_hbm, fwd, const_sem.at[0]),
        pltpu.make_async_copy(inv_hbm, inv, const_sem.at[1]),
    ]
    for copy in consts:
        copy.start()

    barrier = pltpu.get_barrier_semaphore()
    greet = [place(((z + d) % 8) * 16 + e_me, x) for d in range(1, 8)]
    greet += [place(z * 16 + (e_me + d) % 16, x) for d in range(1, 16)]
    greet += [place(tm, (x + d) % 4) for d in range(1, 4)]
    for d in (-2, -1, 1, 2):
        greet.append(place(at_strip(g + d), x))
    for d in (-1, 1):
        for s in (up, down):
            greet.append(place(at_strip(g + d), s))
    for device in greet:
        pl.semaphore_signal(barrier, inc=1, device_id=device, device_id_type=MESH)

    for zz in range(8):
        value = None
        for t in range(4):
            piece = turn(b_ref[t, :, (zz // 4) * 128 : (zz // 4) * 128 + 128], t * 32 - (zz % 4) * 32)
            value = piece if value is None else jnp.where(lane_block(t), piece, value)
        m1[zz] = value
    h[...] = jnp.zeros_like(h)
    wa[...] = jnp.zeros_like(wa)
    wb[...] = jnp.zeros_like(wb)
    r1[z] = m1[z]
    cd[1] = diff_ref[...]
    cv[1] = vel_ref[...]

    pl.semaphore_wait(barrier, len(greet))

    started = []

    def send(src, dst, s_sem, r_sem, device):
        copy = pltpu.make_async_remote_copy(
            src_ref=src, dst_ref=dst, send_sem=s_sem, recv_sem=r_sem, device_id=device, device_id_type=MESH
        )
        copy.start()
        started.append(copy)
        return copy

    stage1 = [
        send(m1.at[(z + d) % 8], r1.at[z], s1_s.at[d], s1_r.at[d], place(((z + d) % 8) * 16 + e_me, x))
        for d in range(1, 8)
    ]
    coefs = [
        send(diff_ref, cd.at[2], coef_s.at[0], coef_r.at[0], place(tm, up)),
        send(vel_ref, cv.at[2], coef_s.at[1], coef_r.at[1], place(tm, up)),
        send(diff_ref, cd.at[0], coef_s.at[2], coef_r.at[2], place(tm, down)),
        send(vel_ref, cv.at[0], coef_s.at[3], coef_r.at[3], place(tm, down)),
    ]
    for copy in stage1:
        copy.wait_recv()
    half = lanes_below(64, (16, 128))
    turned = jnp.transpose(r1[...].reshape(64, 128))
    buf1[:, 0:64] = turned
    for t in range(4):
        even = buf1[pl.ds(t * 32, 16, stride=2), :]
        other = buf1[pl.ds(t * 32 + 1, 16, stride=2), :]
        m2[:, t, :] = jnp.where(half, even, pltpu.roll(other, 64, 1))

    def strip_of(e):
        yy = e // 2
        return (yy + odd * (7 - 2 * yy)) * 2 + e % 2

    r2[e_me] = m2[strip_of(e_me)]
    stage2 = []
    for d in range(1, 16):
        to = (e_me + d) % 16
        stage2.append(
            send(m2.at[strip_of(to)], r2.at[e_me], s2_s.at[d], s2_r.at[d], place(z * 16 + to, x))
        )

    for copy in coefs:
        copy.wait_recv()
    parts = []
    for prev, mine, after in (
        (cd[0], cd[1], cd[2]),
        (cv[0, 0], cv[1, 0], cv[2, 0]),
        (cv[0, 1], cv[1, 1], cv[2, 1]),
    ):
        parts += [prev[4:8], mine, after[0:4]]
    stacked = jnp.concatenate(parts, axis=0)
    row_at = lax.broadcasted_iota(jnp.int32, (256, 128), 0)
    for j in range(8):
        pick = jnp.where(row_at == 2 * g - 3 + j, 1.0, 0.0).astype(F32)
        spread = jnp.dot(stacked, pick, precision=HIGHEST, preferred_element_type=F32)
        diff = spread[0:16]
        v_col = spread[16:32]
        v_row = spread[32:48]
        diag = 1.0 + 4.0 * diff
        point[0, j] = diag
        point[1, j] = -diff - v_row
        point[2, j] = -diff + v_row
        point[3, j] = -diff - v_col
        point[4, j] = -diff + v_col
        row = 8 * x - 4 + lax.broadcasted_iota(jnp.int32, (16, 128), 0)
        column = 2 * g - 3 + j
        inside = (row >= 0) & (row < 32) & (column >= 0) & (column < 256)
        for q in range(2):
            d_i = small_ref[4 + q : 5 + q, :]
            for which, base in ((0, 0), (1, 2)):
                d_r = diag - small_ref[base + q : base + q + 1, :]
                scale = jnp.where(inside, DAMPING / (d_r * d_r + d_i * d_i), 0.0)
                lead[which, q, j] = d_r * scale
                if which == 0:
                    lead[2, q, j] = d_i * scale

    for copy in stage2:
        copy.wait_recv()
    turned = jnp.transpose(r2[...].reshape(64, 128))
    low64 = lanes_below(64)
    tiles = []
    for cl in range(2):
        row = []
        for a in range(4):
            v0 = turned[cl * 64 + a * 16 : cl * 64 + a * 16 + 8, :]
            v1 = turned[cl * 64 + a * 16 + 8 : cl * 64 + a * 16 + 16, :]
            row.append(jnp.concatenate([v0, v1], axis=1))
        tiles.append(jnp.concatenate(row, axis=1))
    field = jnp.concatenate(tiles, axis=0)
    for copy in consts:
        copy.wait()
    spectrum = jnp.dot(field, fwd[...], precision=HIGHEST, preferred_element_type=F32)
    vectors = [field]
    directions = []

    def dot_pairs(a, b):
        high = low = None
        for cl in range(2):
            for q in range(4):
                va = a[cl * 8 : cl * 8 + 8, q * 128 : q * 128 + 128]
                vb = b[cl * 8 : cl * 8 + 8, q * 128 : q * 128 + 128]
                p, e = two_prod(va, vb)
                if high is None:
                    high, low = p, e
                else:
                    high, t = two_sum(high, p)
                    low = low + (t + e)
        for shift in (4, 2, 1):
            high, t = two_sum(high, pltpu.roll(high, shift, 0))
            low = low + pltpu.roll(low, shift, 0) + t
        return high, low

    grams = {}

    def put_spectrum(it, value):
        for q in range(4):
            for cl in range(2):
                own[it, q, cl] = value[cl * 8 : cl * 8 + 8, q * 128 : q * 128 + 128]
                edge4[it, 0, q, cl] = value[cl * 8 : cl * 8 + 4, q * 128 : q * 128 + 128]
                edge4[it, 1, q, cl] = value[cl * 8 + 4 : cl * 8 + 8, q * 128 : q * 128 + 128]
                edge2[it, 0, q, cl] = value[cl * 8 : cl * 8 + 2, q * 128 : q * 128 + 128]
                edge2[it, 1, q, cl] = value[cl * 8 + 6 : cl * 8 + 8, q * 128 : q * 128 + 128]

    def send_halo(it):
        n1, n2, p1, p2 = (at_strip(g - 1), at_strip(g - 2), at_strip(g + 1), at_strip(g + 2))
        moves = (
            (edge2.at[it, 1], nw.at[it], place(p1, down)),
            (edge2.at[it, 1], ne.at[it], place(n1, down)),
            (edge2.at[it, 0], sw.at[it], place(p1, up)),
            (edge2.at[it, 0], se.at[it], place(n1, up)),
            (own.at[it], left1.at[it], place(p1, x)),
            (own.at[it], right1.at[it], place(n1, x)),
            (edge4.at[it, 1], north.at[it], place(tm, down)),
            (edge4.at[it, 0], south.at[it], place(tm, up)),
            (own.at[it, :, 1], left2.at[it], place(p2, x)),
            (own.at[it, :, 0], right2.at[it], place(n2, x)),
        )
        return [
            send(src, dst, ha_s.at[it, i], ha_r.at[it, i], device)
            for i, (src, dst, device) in enumerate(moves)
        ]

    def shifts(q):
        return (small_ref[q : q + 1, :], small_ref[2 + q : 3 + q, :], small_ref[4 + q : 5 + q, :])

    def stencil(w, q, j, start, rows, at):
        here = w[q, j, pl.ds(start, rows), :]
        return here, (
            point[0, j, pl.ds(at, rows), :] * here
            + point[1, j, pl.ds(at, rows), :] * w[q, j, pl.ds(start - 1, rows), :]
            + point[2, j, pl.ds(at, rows), :] * w[q, j, pl.ds(start + 1, rows), :]
            + point[3, j, pl.ds(at, rows), :] * w[q, j - 1, pl.ds(start, rows), :]
            + point[4, j, pl.ds(at, rows), :] * w[q, j + 1, pl.ds(start, rows), :]
        )

    def sweep(source, target, first, last):
        def body(j, carry):
            for at in (0, 8):
                for q in range(2):
                    s_re, s_im, s_x = shifts(q)
                    w_re, b_re = stencil(source, q, j, 8 + at, 8, at)
                    w_im, b_im = stencil(source, q + 2, j, 8 + at, 8, at)
                    rows = pl.ds(at, 8)
                    left_re = h[q, j, rows, :] - (b_re - (s_re * w_re + s_x * w_im))
                    left_im = h[q + 2, j, rows, :] - (b_im - (s_im * w_im - s_x * w_re))
                    p_re, p_im, p_x = lead[0, q, j, rows, :], lead[1, q, j, rows, :], lead[2, q, j, rows, :]
                    target[q, j, pl.ds(8 + at, 8), :] = w_re + (p_re * left_re + p_x * left_im)
                    target[q + 2, j, pl.ds(8 + at, 8), :] = w_im + (p_im * left_im - p_x * left_re)
            return carry

        lax.fori_loop(first, last, body, 0)

    put_spectrum(0, spectrum)
    halo = send_halo(0)
    grams[0, 0] = dot_pairs(field, field)

    for it in range(KRYLOV):
        for q in range(4):
            for cl in range(2):
                h[q, 3 + cl, 4:12, :] = own[it, q, cl]
        for copy in halo:
            copy.wait_recv()
        for q in range(4):
            h[q, 0, 4:12, :] = left2[it, q]
            h[q, 7, 4:12, :] = right2[it, q]
            for cl in range(2):
                h[q, 1 + cl, 4:12, :] = left1[it, q, cl]
                h[q, 1 + cl, 2:4, :] = nw[it, q, cl]
                h[q, 1 + cl, 12:14, :] = sw[it, q, cl]
                h[q, 5 + cl, 4:12, :] = right1[it, q, cl]
                h[q, 5 + cl, 2:4, :] = ne[it, q, cl]
                h[q, 5 + cl, 12:14, :] = se[it, q, cl]
                h[q, 3 + cl, 0:4, :] = north[it, q, cl]
                h[q, 3 + cl, 12:16, :] = south[it, q, cl]

        def first_guess(j, carry):
            for at in (0, 8):
                rows = pl.ds(at, 8)
                for q in range(2):
                    re, im = h[q, j, rows, :], h[q + 2, j, rows, :]
                    p_re, p_im, p_x = lead[0, q, j, rows, :], lead[1, q, j, rows, :], lead[2, q, j, rows, :]
                    wa[q, j, pl.ds(8 + at, 8), :] = p_re * re + p_x * im
                    wa[q + 2, j, pl.ds(8 + at, 8), :] = p_im * im - p_x * re
            return carry

        lax.fori_loop(0, 8, first_guess, 0)
        sweep(wa, wb, 1, 7)
        sweep(wb, wa, 2, 6)
        guess, image = [], []
        for cl in range(2):
            j = 3 + cl
            w_row, g_row = [None] * 4, [None] * 4
            for q in range(2):
                s_re, s_im, s_x = shifts(q)
                w_re, b_re = stencil(wa, q, j, 12, 8, 4)
                w_im, b_im = stencil(wa, q + 2, j, 12, 8, 4)
                w_row[q], w_row[q + 2] = w_re, w_im
                g_row[q] = b_re - (s_re * w_re + s_x * w_im)
                g_row[q + 2] = b_im - (s_im * w_im - s_x * w_re)
            mean = w_row[0] * small_ref[6:7, :]
            for q in range(1, 4):
                mean = mean + w_row[q] * small_ref[6 + q : 7 + q, :]
            corner = jnp.broadcast_to(jnp.sum(mean, axis=1, keepdims=True), (8, 128))
            g_row[0] = g_row[0] + corner
            g_row[1] = g_row[1] + corner
            g_row[2] = g_row[2] + jnp.where(lanes_below(1), corner, 0.0)
            guess.append(jnp.concatenate(w_row, axis=1))
            image.append(jnp.concatenate(g_row, axis=1))
        guess = jnp.concatenate(guess, axis=0)
        image = jnp.concatenate(image, axis=0)
        if it + 1 < KRYLOV:
            put_spectrum(it + 1, image)
            halo = send_halo(it + 1)
        both = jnp.dot(
            jnp.concatenate([guess, image], axis=0), inv[...], precision=HIGHEST, preferred_element_type=F32
        )
        directions.append(both[0:16])
        vectors.append(both[16:32])
        for i in range(it + 2):
            grams[i, it + 1] = dot_pairs(vectors[i], vectors[it + 1])

    order = [(i, j) for i in range(KRYLOV + 1) for j in range(i, KRYLOV + 1)]
    row_is = lax.broadcasted_iota(jnp.int32, (16, 128), 0)
    lane_is = lax.broadcasted_iota(jnp.int32, (16, 128), 1)
    high = jnp.zeros((16, 128), F32)
    low = jnp.zeros((16, 128), F32)
    for n, key in enumerate(order):
        a, b = grams[key]
        high = jnp.where(row_is == n, jnp.concatenate([a, a], axis=0), high)
        low = jnp.where(row_is == n, jnp.concatenate([b, b], axis=0), low)
    for shift in (64, 32, 16, 8, 4, 2, 1):
        high, t = two_sum(high, pltpu.roll(high, shift, 1))
        low = low + pltpu.roll(low, shift, 1) + t
    packed = jnp.where(lane_is == row_is, high, jnp.where(lane_is == row_is + 16, low, 0.0))
    mine = jnp.sum(packed, axis=0, keepdims=True)

    def all_add(mine, src, dst, s_sem, r_sem, devices, me):
        count = len(devices) + 1
        src[...] = mine
        dst[me] = mine
        copies = [
            send(src, dst.at[me], s_sem.at[d], r_sem.at[d], device)
            for d, device in enumerate(devices, start=1)
        ]
        for copy in copies:
            copy.wait_recv()
        level = [(dst[i], None) for i in range(count)]
        while len(level) > 1:
            following = []
            for (a, ea), (b, eb) in zip(level[::2], level[1::2]):
                s, t = two_sum(a, b)
                for extra in (ea, eb):
                    t = t if extra is None else t + extra
                following.append((s, t))
            level = following
        s, t = level[0]
        lane = lax.broadcasted_iota(jnp.int32, (1, 128), 1)
        return s + jnp.where((lane >= 16) & (lane < 32), pltpu.roll(t, 16, 1), 0.0)

    mine = all_add(
        mine, ars0, ar0, a0_s, a0_r, [place(z * 16 + (e_me + d) % 16, x) for d in range(1, 16)], e_me
    )
    mine = all_add(
        mine, ars1, ar1, a1_s, a1_r, [place(((z + d) % 8) * 16 + e_me, x) for d in range(1, 8)], z
    )
    mine = all_add(mine, ars2, ar2, a2_s, a2_r, [place(tm, (x + d) % 4) for d in range(1, 4)], x)
    mine = jnp.broadcast_to(mine, (8, 128))
    gram = [[None] * (KRYLOV + 1) for _ in range(KRYLOV + 1)]
    for n, (i, j) in enumerate(order):
        value = (
            jnp.broadcast_to(mine[:, n : n + 1], (8, 128)),
            jnp.broadcast_to(mine[:, 16 + n : 17 + n], (8, 128)),
        )
        gram[i][j] = value
        gram[j][i] = value
    on_directions, on_vectors = krylov_weights(gram)

    def combined(weights, fields, cl, q):
        total = None
        for weight, value in zip(weights, fields):
            term = weight * value[cl * 8 : cl * 8 + 8, q * 128 : q * 128 + 128]
            total = term if total is None else total + term
        return total

    rows = []
    for cl in range(2):
        for a in range(4):
            f0 = combined(on_directions, directions, cl, a)
            f1 = combined(on_vectors, vectors, cl, a)
            rows.append(jnp.where(low64, f0, pltpu.roll(f1, 64, 1)))
            rows.append(jnp.where(low64, pltpu.roll(f0, 64, 1), f1))
    turned = jnp.transpose(jnp.concatenate(rows, axis=0))
    for src in range(16):
        for f in range(2):
            m3[src, f * 4 : f * 4 + 4, :] = turned[f * 64 + src * 4 : f * 64 + src * 4 + 4, :]
    strip_me = strip_of(e_me)
    r3[strip_me] = m3[e_me]
    stage3 = []
    for d in range(1, 16):
        to = (e_me + d) % 16
        stage3.append(send(m3.at[to], r3.at[strip_me], s3_s.at[d], s3_r.at[d], place(z * 16 + to, x)))
    for copy in stage3:
        copy.wait_recv()
    for t in range(4):
        f0 = r3[:, t, :]
        f1 = r3[:, 4 + t, :]
        buf2[pl.ds(t * 32, 16, stride=2), :] = jnp.where(half, f0, pltpu.roll(f1, 64, 1))
        buf2[pl.ds(t * 32 + 1, 16, stride=2), :] = jnp.where(half, pltpu.roll(f0, 64, 1), f1)
    turned = jnp.transpose(buf2[...])
    for zz in range(8):
        for f in range(2):
            m4[zz, f] = turned[f * 64 + zz * 8 : f * 64 + zz * 8 + 8, :]
    r4[z] = m4[z]
    stage4 = [
        send(m4.at[(z + d) % 8], r4.at[z], s4_s.at[d], s4_r.at[d], place(((z + d) % 8) * 16 + e_me, x))
        for d in range(1, 8)
    ]
    for copy in stage4:
        copy.wait_recv()
    for f, out in ((0, sol_ref), (1, res_ref)):
        for t in range(4):
            for hh in range(2):
                value = None
                for k in range(4):
                    piece = turn(r4[hh * 4 + k, f], k * 32 - t * 32)
                    value = piece if value is None else jnp.where(lane_block(k), piece, value)
                out[t, :, hh * 128 : hh * 128 + 128] = value
    for copy in started:
        copy.wait_send()


def per_device(right_side, diffusion, velocity):
    forward, inverse, small = tables()
    vmem = pl.BlockSpec(memory_space=pltpu.VMEM)
    anywhere = pl.BlockSpec(memory_space=pl.ANY)

    def buffer(*shape):
        return pltpu.VMEM(shape, F32)

    def sems(*shape):
        return pltpu.SemaphoreType.DMA(shape)

    out = jax.ShapeDtypeStruct(right_side.shape, F32)
    return pl.pallas_call(
        kernel,
        out_shape=(out, out),
        in_specs=[vmem, vmem, vmem, vmem, anywhere, anywhere],
        out_specs=(vmem, vmem),
        scratch_shapes=[
            buffer(L, L), buffer(L, L),
            buffer(8, 8, 128), buffer(8, 8, 128), buffer(128, 128), buffer(16, 4, 128), buffer(16, 4, 128),
            buffer(3, 8, 256), buffer(3, 2, 8, 256),
            buffer(5, 8, 16, 128), buffer(3, 2, 8, 16, 128),
            buffer(3, 4, 2, 8, 128), buffer(3, 2, 4, 2, 4, 128), buffer(3, 2, 4, 2, 2, 128),
            buffer(4, 8, 16, 128),
            buffer(3, 4, 2, 8, 128), buffer(3, 4, 2, 8, 128), buffer(3, 4, 8, 128), buffer(3, 4, 8, 128),
            buffer(3, 4, 2, 4, 128), buffer(3, 4, 2, 4, 128),
            buffer(3, 4, 2, 2, 128), buffer(3, 4, 2, 2, 128), buffer(3, 4, 2, 2, 128), buffer(3, 4, 2, 2, 128),
            buffer(4, 8, 32, 128), buffer(4, 8, 32, 128),
            buffer(16, 1, 128), buffer(8, 1, 128), buffer(4, 1, 128),
            buffer(1, 128), buffer(1, 128), buffer(1, 128),
            buffer(16, 8, 128), buffer(16, 8, 128), buffer(128, 128),
            buffer(8, 2, 8, 128), buffer(8, 2, 8, 128),
            sems(2), sems(4), sems(4), sems(8), sems(8), sems(16), sems(16), sems(3, 10), sems(3, 10),
            sems(16), sems(16), sems(8), sems(8), sems(4), sems(4), sems(16), sems(16), sems(8), sems(8),
        ],
        compiler_params=pltpu.CompilerParams(
            collective_id=0, has_side_effects=True, vmem_limit_bytes=32 * 1024 * 1024
        ),
    )(right_side, diffusion, velocity, small, forward, inverse)


def solution(mesh):
    return jax.shard_map(
        per_device,
        mesh=mesh,
        in_specs=(P("tm", "space", None), P("space", None), P(None, "space", None)),
        out_specs=(P("tm", "space", None), P("tm", "space", None)),
        check_vma=False,
    )
```

time: 595 us -> 73.3 us (0.12); the launches traced: 585 us -> 72.9 us
  blocking collectives: 258 us -> 0 us
  starting transfers between devices: 121 us -> 0 us
  waiting for transfers between devices: 78.4 us -> 0 us
  Pallas kernels: 0 us -> 65.7 us
  matrix products: 59.6 us -> 0 us
  other arithmetic: 33.8 us -> 0 us
  local copies, waits for them, and re-layouts: 22.3 us -> 6.54 us
  between operations: 11.6 us -> 0.65 us
    psum x16 -> x0, blocking collectives: 194 us -> none  [one_axis_at_a_time(): value = lax.psum(value, axis)]
    ppermute x33 -> x0, starting transfers between devices: 80.3 us -> none  [the longest x12 34.1 us: extended_2(): lax.ppermute(last, axis, up)]
    pallas_call x0 -> x1, Pallas kernels: none -> 65.7 us  [per_device(): pl.pallas_call(kernel, out_shape=(out, out), in_specs=[vmem, vmem, vmem,...]
    all_to_all x5 -> x0, blocking collectives: 64 us -> none  [the longest x4 34.3 us: turned_blocks(): out = lax.all_to_all(out, axes[k], k, k, tiled=True)]
    all_to_all x4 -> x0, waiting for transfers between devices: 59.7 us -> none  [the longest x2 39.5 us: per_device(): lax.all_to_all(moved, TM, split_axis=1, concat_axis=2, tiled=True)]
    dot_general x12 -> x0, matrix products: 59.6 us -> none  [the longest x3 16 us: forward(): imag_part = -jnp.dot(block, sine, precision=highest)]
    all_to_all x4 -> x0, starting transfers between devices: 40.8 us -> none  [the longest x2 22.6 us: turned_blocks(): out = lax.all_to_all(out, axes[k], k, k, tiled=True)]
    ppermute x33 -> x0, waiting for transfers between devices: 18.7 us -> none  [the longest x12 16.8 us: extended_2(): lax.ppermute(first, axis, [(b, a) for a, b in up])]
  transfers between devices with their start and end apart: 37 -> 0, of which waited for: 13 -> 0; matrix products, arithmetic and copies ran while one was open for 1% -> 0% of each run, Pallas kernels for 0% -> 0%
where the time goes in v1:
time: 73.3 us; the launch traced here: 72.9 us
  Pallas kernels  65.7 us (90%)
  local copies, waits for them, and re-layouts  6.54 us (9%)
    pallas_call x1, Pallas kernels, per_device(): pl.pallas_call(kernel, out_shape=(out, out), in_specs=[vmem, vmem, vmem,...  65.7 us
    unnamed x14, local copies, waits for them, and re-layouts  6.54 us

profile of v1, /device:TPU:1, one launch (start us, length us, event | category | flops | bytes accessed | tf_op | source)
XLA Modules:
  0.0 72.9 jit_solution(8768201100204618493)
XLA Ops:
  0.6 0.0 copy-start
  0.6 1.2 %copy-done = f32[512,512]{1,0:T(8,128)S(1)} copy-done((f32[512,512]{1,0:T(8,128)S(1)}, f32[512,512]{1,0:T(8,128)}, u32[]{:S(2)}) %copy-start) | copy-done | bytes 1048600
  1.9 0.0 copy-start.1
  1.9 1.2 %copy-done.1 = f32[512,512]{1,0:T(8,128)S(1)} copy-done((f32[512,512]{1,0:T(8,128)S(1)}, f32[512,512]{1,0:T(8,128)}, u32[]{:S(2)}) %copy-start.1) | copy-done | bytes 1048600
  3.1 0.0 copy-start.2
  3.1 0.8 %copy-done.2 = f32[4,8,256]{2,1,0:T(8,128)S(1)} copy-done((f32[4,8,256]{2,1,0:T(8,128)S(1)}, f32[4,8,256]{2,1,0:T(8,128)}, u32[]{:S(2)}) %copy-start.2) | copy-done | bytes 32792
  3.8 0.0 copy-start.3
  3.8 0.7 copy-done.3
  4.6 0.0 copy-start.4
  4.6 0.7 copy-done.4
  5.3 0.0 copy-start.5
  5.3 0.7 copy-done.5
  6.0 65.7 %shard_map.77 = (f32[4,8,256]{2,1,0:T(8,128)S(1)}, f32[4,8,256]{2,1,0:T(8,128)S(1)}) custom-call(f32[4,8,256]{2,1,0:T(8,128)S(1)} %copy-done.2, f32[8,256]{1,0:T(8,128)S(1)} %copy-done.4, f32[2,8,256]{2,1,0:T(8,128)S(1)} %copy-done.3, f32[16,128]{1,0:T(8,128)S(1)} %copy-done.5, f32[512,512]{1,0:T(8,128)S(1)} %copy-done.1, f32[512,512]{1,0:T(8,128)S(1)} %copy-done), custom_call_target="tpu_custom_call" | custom-call | tf_op jit(solution)/shard_map/pallas_call | solution.py:618
  71.6 0.6 copy.10
  72.2 0.6 copy.11
Async XLA Ops:
  0.6 1.2 %copy-start = (f32[512,512]{1,0:T(8,128)S(1)}, f32[512,512]{1,0:T(8,128)}, u32[]{:S(2)}) copy-start(f32[512,512]{1,0:T(8,128)} %constant.8.clone.inv_hbm) | copy-start | bytes 3145732
  1.9 1.2 %copy-start.1 = (f32[512,512]{1,0:T(8,128)S(1)}, f32[512,512]{1,0:T(8,128)}, u32[]{:S(2)}) copy-start(f32[512,512]{1,0:T(8,128)} %constant.7.clone.fwd_hbm) | copy-start | bytes 3145732
  3.1 0.8 %copy-start.2 = (f32[4,8,256]{2,1,0:T(8,128)S(1)}, f32[4,8,256]{2,1,0:T(8,128)}, u32[]{:S(2)}) copy-start(f32[4,8,256]{2,1,0:T(8,128)} %b_ref.1) | copy-start | bytes 98308
  3.8 0.7 copy-start.3
  4.6 0.7 copy-start.4
  5.3 0.7 copy-start.5

commit v2 on v1

--- a/solution.py
+++ b/solution.py
@@ -17,6 +17,8 @@
 DECAY = math.exp(LOG_DECAY)
 MESH = pl.DeviceIdType.MESH
 HIGHEST = lax.Precision.HIGHEST
+FAR_8 = (4, 3, 5, 2, 6, 1, 7)
+FAR_16 = (8, 7, 9, 6, 10, 5, 11, 4, 12, 3, 13, 2, 14, 1, 15)
 F32 = jnp.float32
 
 
@@ -185,9 +187,9 @@
 
 
 def kernel(
-    b_ref, diff_ref, vel_ref, small_ref, fwd_hbm, inv_hbm,
+    b_hbm, diff_hbm, vel_hbm, small_hbm, fwd_hbm, inv_hbm,
     sol_ref, res_ref,
-    fwd, inv,
+    b_ref, diff_ref, vel_ref, small_ref, fwd, inv,
     m1, r1, buf1, m2, r2, cd, cv, point, lead, own, edge4, edge2, h,
     left1, right1, left2, right2, north, south, nw, ne, sw, se, wa, wb,
     ar0, ar1, ar2, ars0, ars1, ars2, m3, r3, buf2, m4, r4,
@@ -217,16 +219,19 @@
 
     up = (x + 3) % 4
     down = (x + 1) % 4
-    consts = [
-        pltpu.make_async_copy(fwd_hbm, fwd, const_sem.at[0]),
-        pltpu.make_async_copy(inv_hbm, inv, const_sem.at[1]),
+    loads = [
+        pltpu.make_async_copy(src, dst, const_sem.at[i])
+        for i, (src, dst) in enumerate(
+            (
+                (b_hbm, b_ref), (diff_hbm, diff_ref), (vel_hbm, vel_ref),
+                (small_hbm, small_ref), (fwd_hbm, fwd), (inv_hbm, inv),
+            )
+        )
     ]
-    for copy in consts:
-        copy.start()
-
+    loads[0].start()
     barrier = pltpu.get_barrier_semaphore()
-    greet = [place(((z + d) % 8) * 16 + e_me, x) for d in range(1, 8)]
-    greet += [place(z * 16 + (e_me + d) % 16, x) for d in range(1, 16)]
+    greet = [place(((z + d) % 8) * 16 + e_me, x) for d in FAR_8]
+    greet += [place(z * 16 + (e_me + d) % 16, x) for d in FAR_16]
     greet += [place(tm, (x + d) % 4) for d in range(1, 4)]
     for d in (-2, -1, 1, 2):
         greet.append(place(at_strip(g + d), x))
@@ -235,6 +240,9 @@
             greet.append(place(at_strip(g + d), s))
     for device in greet:
         pl.semaphore_signal(barrier, inc=1, device_id=device, device_id_type=MESH)
+    for copy in loads[1:]:
+        copy.start()
+    loads[0].wait()
 
     for zz in range(8):
         value = None
@@ -242,12 +250,9 @@
             piece = turn(b_ref[t, :, (zz // 4) * 128 : (zz // 4) * 128 + 128], t * 32 - (zz % 4) * 32)
             value = piece if value is None else jnp.where(lane_block(t), piece, value)
         m1[zz] = value
-    h[...] = jnp.zeros_like(h)
-    wa[...] = jnp.zeros_like(wa)
-    wb[...] = jnp.zeros_like(wb)
     r1[z] = m1[z]
-    cd[1] = diff_ref[...]
-    cv[1] = vel_ref[...]
+    loads[1].wait()
+    loads[2].wait()
 
     pl.semaphore_wait(barrier, len(greet))
 
@@ -263,7 +268,7 @@
 
     stage1 = [
         send(m1.at[(z + d) % 8], r1.at[z], s1_s.at[d], s1_r.at[d], place(((z + d) % 8) * 16 + e_me, x))
-        for d in range(1, 8)
+        for d in FAR_8
     ]
     coefs = [
         send(diff_ref, cd.at[2], coef_s.at[0], coef_r.at[0], place(tm, up)),
@@ -271,6 +276,12 @@
         send(diff_ref, cd.at[0], coef_s.at[2], coef_r.at[2], place(tm, down)),
         send(vel_ref, cv.at[0], coef_s.at[3], coef_r.at[3], place(tm, down)),
     ]
+    h[...] = jnp.zeros_like(h)
+    wa[...] = jnp.zeros_like(wa)
+    wb[...] = jnp.zeros_like(wb)
+    cd[1] = diff_ref[...]
+    cv[1] = vel_ref[...]
+    loads[3].wait()
     for copy in stage1:
         copy.wait_recv()
     half = lanes_below(64, (16, 128))
@@ -287,7 +298,7 @@
 
     r2[e_me] = m2[strip_of(e_me)]
     stage2 = []
-    for d in range(1, 16):
+    for d in FAR_16:
         to = (e_me + d) % 16
         stage2.append(
             send(m2.at[strip_of(to)], r2.at[e_me], s2_s.at[d], s2_r.at[d], place(z * 16 + to, x))
@@ -341,8 +352,8 @@
             row.append(jnp.concatenate([v0, v1], axis=1))
         tiles.append(jnp.concatenate(row, axis=1))
     field = jnp.concatenate(tiles, axis=0)
-    for copy in consts:
-        copy.wait()
+    loads[4].wait()
+    loads[5].wait()
     spectrum = jnp.dot(field, fwd[...], precision=HIGHEST, preferred_element_type=F32)
     vectors = [field]
     directions = []
@@ -423,6 +434,53 @@
             return carry
 
         lax.fori_loop(first, last, body, 0)
+
+    strip_me = strip_of(e_me)
+    stage3, stage4 = {}, {}
+
+    def pieces(value):
+        return [[value[cl * 8 : cl * 8 + 8, q * 128 : q * 128 + 128] for q in range(4)] for cl in range(2)]
+
+    def send_strip(it):
+        p0, p1 = pieces(directions[it]), pieces(vectors[it + 1])
+        rows = []
+        for cl in range(2):
+            for a in range(4):
+                f0, f1 = p0[cl][a], p1[cl][a]
+                rows.append(jnp.where(low64, f0, pltpu.roll(f1, 64, 1)))
+                rows.append(jnp.where(low64, pltpu.roll(f0, 64, 1), f1))
+        turned = jnp.transpose(jnp.concatenate(rows, axis=0))
+        for src in range(16):
+            for f in range(2):
+                m3[it, src, f * 4 : f * 4 + 4, :] = turned[f * 64 + src * 4 : f * 64 + src * 4 + 4, :]
+        r3[it, strip_me] = m3[it, e_me]
+        stage3[it] = []
+        for d in FAR_16:
+            to = (e_me + d) % 16
+            stage3[it].append(
+                send(m3.at[it, to], r3.at[it, strip_me], s3_s.at[it, d], s3_r.at[it, d], place(z * 16 + to, x))
+            )
+
+    def send_steps(it):
+        for copy in stage3[it]:
+            copy.wait_recv()
+        for t in range(4):
+            f0 = r3[it, :, t, :]
+            f1 = r3[it, :, 4 + t, :]
+            buf2[pl.ds(t * 32, 16, stride=2), :] = jnp.where(half, f0, pltpu.roll(f1, 64, 1))
+            buf2[pl.ds(t * 32 + 1, 16, stride=2), :] = jnp.where(half, pltpu.roll(f0, 64, 1), f1)
+        turned = jnp.transpose(buf2[...])
+        for zz in range(8):
+            for f in range(2):
+                m4[it, zz, f] = turned[f * 64 + zz * 8 : f * 64 + zz * 8 + 8, :]
+        r4[it, z] = m4[it, z]
+        stage4[it] = [
+            send(
+                m4.at[it, (z + d) % 8], r4.at[it, z], s4_s.at[it, d], s4_r.at[it, d],
+                place(((z + d) % 8) * 16 + e_me, x),
+            )
+            for d in FAR_8
+        ]
 
     put_spectrum(0, spectrum)
     halo = send_halo(0)
@@ -490,8 +548,11 @@
         )
         directions.append(both[0:16])
         vectors.append(both[16:32])
+        send_strip(it)
         for i in range(it + 2):
             grams[i, it + 1] = dot_pairs(vectors[i], vectors[it + 1])
+        if it == 1:
+            send_steps(0)
 
     order = [(i, j) for i in range(KRYLOV + 1) for j in range(i, KRYLOV + 1)]
     row_is = lax.broadcasted_iota(jnp.int32, (16, 128), 0)
@@ -508,17 +569,15 @@
     packed = jnp.where(lane_is == row_is, high, jnp.where(lane_is == row_is + 16, low, 0.0))
     mine = jnp.sum(packed, axis=0, keepdims=True)
 
-    def all_add(mine, src, dst, s_sem, r_sem, devices, me):
-        count = len(devices) + 1
+    def add_start(mine, src, dst, s_sem, r_sem, devices, me):
         src[...] = mine
         dst[me] = mine
-        copies = [
-            send(src, dst.at[me], s_sem.at[d], r_sem.at[d], device)
-            for d, device in enumerate(devices, start=1)
-        ]
+        return [send(src, dst.at[me], s_sem.at[d], r_sem.at[d], device) for d, device in devices]
+
+    def add_end(copies, dst):
         for copy in copies:
             copy.wait_recv()
-        level = [(dst[i], None) for i in range(count)]
+        level = [(dst[i], None) for i in range(len(copies) + 1)]
         while len(level) > 1:
             following = []
             for (a, ea), (b, eb) in zip(level[::2], level[1::2]):
@@ -531,13 +590,16 @@
         lane = lax.broadcasted_iota(jnp.int32, (1, 128), 1)
         return s + jnp.where((lane >= 16) & (lane < 32), pltpu.roll(t, 16, 1), 0.0)
 
-    mine = all_add(
-        mine, ars0, ar0, a0_s, a0_r, [place(z * 16 + (e_me + d) % 16, x) for d in range(1, 16)], e_me
+    adds = add_start(
+        mine, ars1, ar1, a1_s, a1_r, [(d, place(((z + d) % 8) * 16 + e_me, x)) for d in FAR_8], z
     )
-    mine = all_add(
-        mine, ars1, ar1, a1_s, a1_r, [place(((z + d) % 8) * 16 + e_me, x) for d in range(1, 8)], z
-    )
-    mine = all_add(mine, ars2, ar2, a2_s, a2_r, [place(tm, (x + d) % 4) for d in range(1, 4)], x)
+    send_steps(1)
+    mine = add_end(adds, ar1)
+    adds = add_start(mine, ars0, ar0, a0_s, a0_r, [(d, place(z * 16 + (e_me + d) % 16, x)) for d in FAR_16], e_me)
+    send_steps(2)
+    mine = add_end(adds, ar0)
+    adds = add_start(mine, ars2, ar2, a2_s, a2_r, [(d, place(tm, (x + d) % 4)) for d in (2, 1, 3)], x)
+    mine = add_end(adds, ar2)
     mine = jnp.broadcast_to(mine, (8, 128))
     gram = [[None] * (KRYLOV + 1) for _ in range(KRYLOV + 1)]
     for n, (i, j) in enumerate(order):
@@ -549,54 +611,25 @@
         gram[j][i] = value
     on_directions, on_vectors = krylov_weights(gram)
 
-    def combined(weights, fields, cl, q):
-        total = None
-        for weight, value in zip(weights, fields):
-            term = weight * value[cl * 8 : cl * 8 + 8, q * 128 : q * 128 + 128]
-            total = term if total is None else total + term
-        return total
-
-    rows = []
-    for cl in range(2):
-        for a in range(4):
-            f0 = combined(on_directions, directions, cl, a)
-            f1 = combined(on_vectors, vectors, cl, a)
-            rows.append(jnp.where(low64, f0, pltpu.roll(f1, 64, 1)))
-            rows.append(jnp.where(low64, pltpu.roll(f0, 64, 1), f1))
-    turned = jnp.transpose(jnp.concatenate(rows, axis=0))
-    for src in range(16):
-        for f in range(2):
-            m3[src, f * 4 : f * 4 + 4, :] = turned[f * 64 + src * 4 : f * 64 + src * 4 + 4, :]
-    strip_me = strip_of(e_me)
-    r3[strip_me] = m3[e_me]
-    stage3 = []
-    for d in range(1, 16):
-        to = (e_me + d) % 16
-        stage3.append(send(m3.at[to], r3.at[strip_me], s3_s.at[d], s3_r.at[d], place(z * 16 + to, x)))
-    for copy in stage3:
-        copy.wait_recv()
-    for t in range(4):
-        f0 = r3[:, t, :]
-        f1 = r3[:, 4 + t, :]
-        buf2[pl.ds(t * 32, 16, stride=2), :] = jnp.where(half, f0, pltpu.roll(f1, 64, 1))
-        buf2[pl.ds(t * 32 + 1, 16, stride=2), :] = jnp.where(half, pltpu.roll(f0, 64, 1), f1)
-    turned = jnp.transpose(buf2[...])
+    for it in range(KRYLOV):
+        for copy in stage4[it]:
+            copy.wait_recv()
+    sums = [[], []]
     for zz in range(8):
-        for f in range(2):
-            m4[zz, f] = turned[f * 64 + zz * 8 : f * 64 + zz * 8 + 8, :]
-    r4[z] = m4[z]
-    stage4 = [
-        send(m4.at[(z + d) % 8], r4.at[z], s4_s.at[d], s4_r.at[d], place(((z + d) % 8) * 16 + e_me, x))
-        for d in range(1, 8)
-    ]
-    for copy in stage4:
-        copy.wait_recv()
+        total = on_directions[0] * r4[0, zz, 0]
+        for it in range(1, KRYLOV):
+            total = total + on_directions[it] * r4[it, zz, 0]
+        sums[0].append(total)
+        total = on_vectors[0] * m1[zz]
+        for it in range(KRYLOV):
+            total = total + on_vectors[it + 1] * r4[it, zz, 1]
+        sums[1].append(total)
     for f, out in ((0, sol_ref), (1, res_ref)):
         for t in range(4):
             for hh in range(2):
                 value = None
                 for k in range(4):
-                    piece = turn(r4[hh * 4 + k, f], k * 32 - t * 32)
+                    piece = turn(sums[f][hh * 4 + k], k * 32 - t * 32)
                     value = piece if value is None else jnp.where(lane_block(k), piece, value)
                 out[t, :, hh * 128 : hh * 128 + 128] = value
     for copy in started:
@@ -606,7 +639,7 @@
 def per_device(right_side, diffusion, velocity):
     forward, inverse, small = tables()
     vmem = pl.BlockSpec(memory_space=pltpu.VMEM)
-    anywhere = pl.BlockSpec(memory_space=pl.ANY)
+    hbm = pl.BlockSpec(memory_space=pltpu.HBM)
 
     def buffer(*shape):
         return pltpu.VMEM(shape, F32)
@@ -618,10 +651,10 @@
     return pl.pallas_call(
         kernel,
         out_shape=(out, out),
-        in_specs=[vmem, vmem, vmem, vmem, anywhere, anywhere],
+        in_specs=[hbm] * 6,
         out_specs=(vmem, vmem),
         scratch_shapes=[
-            buffer(L, L), buffer(L, L),
+            buffer(4, 8, 256), buffer(8, 256), buffer(2, 8, 256), buffer(16, 128), buffer(L, L), buffer(L, L),
             buffer(8, 8, 128), buffer(8, 8, 128), buffer(128, 128), buffer(16, 4, 128), buffer(16, 4, 128),
             buffer(3, 8, 256), buffer(3, 2, 8, 256),
             buffer(5, 8, 16, 128), buffer(3, 2, 8, 16, 128),
@@ -633,13 +666,14 @@
             buffer(4, 8, 32, 128), buffer(4, 8, 32, 128),
             buffer(16, 1, 128), buffer(8, 1, 128), buffer(4, 1, 128),
             buffer(1, 128), buffer(1, 128), buffer(1, 128),
-            buffer(16, 8, 128), buffer(16, 8, 128), buffer(128, 128),
-            buffer(8, 2, 8, 128), buffer(8, 2, 8, 128),
-            sems(2), sems(4), sems(4), sems(8), sems(8), sems(16), sems(16), sems(3, 10), sems(3, 10),
-            sems(16), sems(16), sems(8), sems(8), sems(4), sems(4), sems(16), sems(16), sems(8), sems(8),
+            buffer(3, 16, 8, 128), buffer(3, 16, 8, 128), buffer(128, 128),
+            buffer(3, 8, 2, 8, 128), buffer(3, 8, 2, 8, 128),
+            sems(6), sems(4), sems(4), sems(8), sems(8), sems(16), sems(16), sems(3, 10), sems(3, 10),
+            sems(16), sems(16), sems(8), sems(8), sems(4), sems(4),
+            sems(3, 16), sems(3, 16), sems(3, 8), sems(3, 8),
         ],
         compiler_params=pltpu.CompilerParams(
-            collective_id=0, has_side_effects=True, vmem_limit_bytes=32 * 1024 * 1024
+            collective_id=0, has_side_effects=True, vmem_limit_bytes=67_000_000
         ),
     )(right_side, diffusion, velocity, small, forward, inverse)
 

time: 73.3 us -> 58.5 us (0.80)
  Pallas kernels: 65.7 us -> 55.7 us
  local copies, waits for them, and re-layouts: 6.54 us -> 2 us
    pallas_call x1, Pallas kernels: 65.7 us -> 55.7 us  [per_device(): pl.pallas_call(kernel, out_shape=(out, out), in_specs=[hbm] * 6, out_spec...]
    unnamed x14 -> x4, local copies, waits for them, and re-layouts: 6.54 us -> 2 us
where the time goes in v2:
time: 58.5 us; the launch traced here: 58.3 us
  Pallas kernels  55.7 us (95%)
  local copies, waits for them, and re-layouts  2 us (3%)
  between operations  0.65 us (1%)
    pallas_call x1, Pallas kernels, per_device(): pl.pallas_call(kernel, out_shape=(out, out), in_specs=[hbm] * 6, out_spec...  55.7 us
    unnamed x4, local copies, waits for them, and re-layouts  2 us

profile of v2, /device:TPU:1, one launch (start us, length us, event | category | flops | bytes accessed | tf_op | source)
XLA Modules:
  0.0 58.3 jit_solution(7766315689513774045)
XLA Ops:
  0.6 55.7 %shard_map.77 = (f32[4,8,256]{2,1,0:T(8,128)}, f32[4,8,256]{2,1,0:T(8,128)}) custom-call(f32[4,8,256]{2,1,0:T(8,128)} %b_hbm.1, f32[8,256]{1,0:T(8,128)} %diff_hbm.1, f32[2,8,256]{2,1,0:T(8,128)} %vel_hbm.1, f32[16,128]{1,0:T(8,128)} %constant.6.clone.small_hbm, f32[512,512]{1,0:T(8,128)} %constant.7.clone.fwd_hbm, f32[512,512]{1,0:T(8,128)} %constant.8.clone.inv_hbm), custom_call_target="tpu_custom_call" | custom-call | tf_op jit(solution)/shard_map/pallas_call | solution.py:651
  56.3 0.0 copy-start
  56.3 1.4 %copy.10 = f32[4,8,256]{2,1,0:T(8,128)} copy(f32[4,8,256]{2,1,0:T(8,128)} %get-tuple-element.4) | data formatting | bytes 65536
  57.7 0.0 copy-done
  57.7 0.6 %copy.11 = f32[4,8,256]{2,1,0:T(8,128)} copy(f32[4,8,256]{2,1,0:T(8,128)S(1)} %copy-done) | data formatting | bytes 65536
Async XLA Ops:
  56.3 1.4 %copy-start = (f32[4,8,256]{2,1,0:T(8,128)S(1)}, f32[4,8,256]{2,1,0:T(8,128)}, u32[]{:S(2)}) copy-start(f32[4,8,256]{2,1,0:T(8,128)} %get-tuple-element.5) | copy-start | bytes 98308

commit v3 on v2

--- a/solution.py
+++ b/solution.py
@@ -18,6 +18,7 @@
 MESH = pl.DeviceIdType.MESH
 HIGHEST = lax.Precision.HIGHEST
 FAR_8 = (4, 3, 5, 2, 6, 1, 7)
+FAR_32 = tuple((d, c) for c in (2, 1, 3, 0) for d in FAR_8 + (0,) if (d, c) != (0, 0))
 FAR_16 = (8, 7, 9, 6, 10, 5, 11, 4, 12, 3, 13, 2, 14, 1, 15)
 F32 = jnp.float32
 
@@ -192,8 +193,8 @@
     b_ref, diff_ref, vel_ref, small_ref, fwd, inv,
     m1, r1, buf1, m2, r2, cd, cv, point, lead, own, edge4, edge2, h,
     left1, right1, left2, right2, north, south, nw, ne, sw, se, wa, wb,
-    ar0, ar1, ar2, ars0, ars1, ars2, m3, r3, buf2, m4, r4,
-    const_sem, coef_s, coef_r, s1_s, s1_r, s2_s, s2_r, ha_s, ha_r, a0_s, a0_r, a1_s, a1_r, a2_s, a2_r,
+    ar0, ar1, ars0, ars1, m3, r3, buf2, m4, r4,
+    const_sem, coef_s, coef_r, s1_s, s1_r, s2_s, s2_r, ha_s, ha_r, a0_s, a0_r, a1_s, a1_r,
     s3_s, s3_r, s4_s, s4_r,
 ):
     tm = lax.axis_index("tm")
@@ -590,16 +591,15 @@
         lane = lax.broadcasted_iota(jnp.int32, (1, 128), 1)
         return s + jnp.where((lane >= 16) & (lane < 32), pltpu.roll(t, 16, 1), 0.0)
 
-    adds = add_start(
-        mine, ars1, ar1, a1_s, a1_r, [(d, place(((z + d) % 8) * 16 + e_me, x)) for d in FAR_8], z
-    )
+    others = [
+        (d * 4 + c, place(((z + d) % 8) * 16 + e_me, (x + c) % 4)) for d, c in FAR_32
+    ]
+    adds = add_start(mine, ars1, ar1, a1_s, a1_r, others, z * 4 + x)
     send_steps(1)
     mine = add_end(adds, ar1)
     adds = add_start(mine, ars0, ar0, a0_s, a0_r, [(d, place(z * 16 + (e_me + d) % 16, x)) for d in FAR_16], e_me)
     send_steps(2)
     mine = add_end(adds, ar0)
-    adds = add_start(mine, ars2, ar2, a2_s, a2_r, [(d, place(tm, (x + d) % 4)) for d in (2, 1, 3)], x)
-    mine = add_end(adds, ar2)
     mine = jnp.broadcast_to(mine, (8, 128))
     gram = [[None] * (KRYLOV + 1) for _ in range(KRYLOV + 1)]
     for n, (i, j) in enumerate(order):
@@ -664,18 +664,17 @@
             buffer(3, 4, 2, 4, 128), buffer(3, 4, 2, 4, 128),
             buffer(3, 4, 2, 2, 128), buffer(3, 4, 2, 2, 128), buffer(3, 4, 2, 2, 128), buffer(3, 4, 2, 2, 128),
             buffer(4, 8, 32, 128), buffer(4, 8, 32, 128),
-            buffer(16, 1, 128), buffer(8, 1, 128), buffer(4, 1, 128),
-            buffer(1, 128), buffer(1, 128), buffer(1, 128),
+            buffer(16, 1, 128), buffer(32, 1, 128), buffer(1, 128), buffer(1, 128),
             buffer(3, 16, 8, 128), buffer(3, 16, 8, 128), buffer(128, 128),
             buffer(3, 8, 2, 8, 128), buffer(3, 8, 2, 8, 128),
             sems(6), sems(4), sems(4), sems(8), sems(8), sems(16), sems(16), sems(3, 10), sems(3, 10),
-            sems(16), sems(16), sems(8), sems(8), sems(4), sems(4),
+            sems(16), sems(16), sems(32), sems(32),
             sems(3, 16), sems(3, 16), sems(3, 8), sems(3, 8),
         ],
         compiler_params=pltpu.CompilerParams(
-            collective_id=0, has_side_effects=True, vmem_limit_bytes=67_000_000
+            collective_id=0, has_side_effects=True, vmem_limit_bytes=40_000_000
         ),
-    )(right_side, diffusion, velocity, small, forward, inverse)
+    )(*[pltpu.with_memory_space_constraint(v, pltpu.HBM) for v in (right_side, diffusion, velocity, jnp.asarray(small), jnp.asarray(forward), jnp.asarray(inverse))])
 
 
 def solution(mesh):

time: 58.5 us -> 56.2 us (0.961)
  Pallas kernels: 55.7 us -> 54.2 us
  local copies, waits for them, and re-layouts: 2 us -> 1.23 us
    pallas_call x1, Pallas kernels: 55.7 us -> 54.2 us  [per_device(): pl.pallas_call(kernel, out_shape=(out, out), in_specs=[hbm] * 6, out_spec...]
    unnamed x4 -> x2, local copies, waits for them, and re-layouts: 2 us -> 1.23 us
where the time goes in v3:
time: 56.2 us; the launch traced here: 56.1 us
  Pallas kernels  54.2 us (96%)
  local copies, waits for them, and re-layouts  1.23 us (2%)
  between operations  0.64 us (1%)
    pallas_call x1, Pallas kernels, per_device(): pl.pallas_call(kernel, out_shape=(out, out), in_specs=[hbm] * 6, out_spec...  54.2 us
    unnamed x2, local copies, waits for them, and re-layouts  1.23 us

profile of v3, /device:TPU:1, one launch (start us, length us, event | category | flops | bytes accessed | tf_op | source)
XLA Modules:
  0.0 56.1 jit_solution(5928331305318945844)
XLA Ops:
  0.6 54.2 %shard_map.77 = (f32[4,8,256]{2,1,0:T(8,128)S(1)}, f32[4,8,256]{2,1,0:T(8,128)S(1)}) custom-call(f32[4,8,256]{2,1,0:T(8,128)} %b_hbm.1, f32[8,256]{1,0:T(8,128)} %diff_hbm.1, f32[2,8,256]{2,1,0:T(8,128)} %vel_hbm.1, f32[16,128]{1,0:T(8,128)} %constant.6.clone.small_hbm, f32[512,512]{1,0:T(8,128)} %constant.7.clone.fwd_hbm, f32[512,512]{1,0:T(8,128)} %constant.8.clone.inv_hbm), custom_call_target="tpu_custom_call" | custom-call | tf_op jit(solution)/shard_map/pallas_call | solution.py:651
  54.8 0.6 %copy.10 = f32[4,8,256]{2,1,0:T(8,128)} copy(f32[4,8,256]{2,1,0:T(8,128)S(1)} %get-tuple-element.4) | data formatting | bytes 65536
  55.4 0.6 %copy.11 = f32[4,8,256]{2,1,0:T(8,128)} copy(f32[4,8,256]{2,1,0:T(8,128)S(1)} %get-tuple-element.5) | data formatting | bytes 65536

commit v4 on v3

--- a/solution.py
+++ b/solution.py
@@ -189,7 +189,7 @@
 
 def kernel(
     b_hbm, diff_hbm, vel_hbm, small_hbm, fwd_hbm, inv_hbm,
-    sol_ref, res_ref,
+    out_ref,
     b_ref, diff_ref, vel_ref, small_ref, fwd, inv,
     m1, r1, buf1, m2, r2, cd, cv, point, lead, own, edge4, edge2, h,
     left1, right1, left2, right2, north, south, nw, ne, sw, se, wa, wb,
@@ -233,9 +233,7 @@
     barrier = pltpu.get_barrier_semaphore()
     greet = [place(((z + d) % 8) * 16 + e_me, x) for d in FAR_8]
     greet += [place(z * 16 + (e_me + d) % 16, x) for d in FAR_16]
-    greet += [place(tm, (x + d) % 4) for d in range(1, 4)]
-    for d in (-2, -1, 1, 2):
-        greet.append(place(at_strip(g + d), x))
+    greet += [place(tm, up), place(tm, down)]
     for d in (-1, 1):
         for s in (up, down):
             greet.append(place(at_strip(g + d), s))
@@ -406,35 +404,54 @@
             for i, (src, dst, device) in enumerate(moves)
         ]
 
-    def shifts(q):
-        return (small_ref[q : q + 1, :], small_ref[2 + q : 3 + q, :], small_ref[4 + q : 5 + q, :])
-
-    def stencil(w, q, j, start, rows, at):
-        here = w[q, j, pl.ds(start, rows), :]
+    shifts = [
+        [jnp.broadcast_to(small_ref[2 * k + q : 2 * k + q + 1, :], (8, 128)) for k in range(3)] for q in range(2)
+    ]
+
+    def weights_of(j, at):
+        return [point[k, j, pl.ds(at, 8), :] for k in range(5)]
+
+    def stencil(w, q, j, start, weights):
+        here = w[q, j, pl.ds(start, 8), :]
         return here, (
-            point[0, j, pl.ds(at, rows), :] * here
-            + point[1, j, pl.ds(at, rows), :] * w[q, j, pl.ds(start - 1, rows), :]
-            + point[2, j, pl.ds(at, rows), :] * w[q, j, pl.ds(start + 1, rows), :]
-            + point[3, j, pl.ds(at, rows), :] * w[q, j - 1, pl.ds(start, rows), :]
-            + point[4, j, pl.ds(at, rows), :] * w[q, j + 1, pl.ds(start, rows), :]
+            weights[0] * here
+            + weights[1] * w[q, j, pl.ds(start - 1, 8), :]
+            + weights[2] * w[q, j, pl.ds(start + 1, 8), :]
+            + weights[3] * w[q, j - 1, pl.ds(start, 8), :]
+            + weights[4] * w[q, j + 1, pl.ds(start, 8), :]
         )
 
     def sweep(source, target, first, last):
         def body(j, carry):
+            done = []
             for at in (0, 8):
+                weights = weights_of(j, at)
                 for q in range(2):
-                    s_re, s_im, s_x = shifts(q)
-                    w_re, b_re = stencil(source, q, j, 8 + at, 8, at)
-                    w_im, b_im = stencil(source, q + 2, j, 8 + at, 8, at)
+                    s_re, s_im, s_x = shifts[q]
+                    w_re, b_re = stencil(source, q, j, 8 + at, weights)
+                    w_im, b_im = stencil(source, q + 2, j, 8 + at, weights)
                     rows = pl.ds(at, 8)
                     left_re = h[q, j, rows, :] - (b_re - (s_re * w_re + s_x * w_im))
                     left_im = h[q + 2, j, rows, :] - (b_im - (s_im * w_im - s_x * w_re))
                     p_re, p_im, p_x = lead[0, q, j, rows, :], lead[1, q, j, rows, :], lead[2, q, j, rows, :]
-                    target[q, j, pl.ds(8 + at, 8), :] = w_re + (p_re * left_re + p_x * left_im)
-                    target[q + 2, j, pl.ds(8 + at, 8), :] = w_im + (p_im * left_im - p_x * left_re)
+                    done.append((q, at, w_re + (p_re * left_re + p_x * left_im)))
+                    done.append((q + 2, at, w_im + (p_im * left_im - p_x * left_re)))
+            for q, at, value in done:
+                target[q, j, pl.ds(8 + at, 8), :] = value
             return carry
 
-        lax.fori_loop(first, last, body, 0)
+        lax.fori_loop(first, last, body, 0, unroll=2)
+
+    def guess_on(j, first, rows):
+        at = pl.ds(first, rows)
+        done = []
+        for q in range(2):
+            re, im = h[q, j, at, :], h[q + 2, j, at, :]
+            p_re, p_im, p_x = lead[0, q, j, at, :], lead[1, q, j, at, :], lead[2, q, j, at, :]
+            done.append((q, p_re * re + p_x * im))
+            done.append((q + 2, p_im * im - p_x * re))
+        for q, value in done:
+            wa[q, j, pl.ds(8 + first, rows), :] = value
 
     strip_me = strip_of(e_me)
     stage3, stage4 = {}, {}
@@ -491,42 +508,45 @@
         for q in range(4):
             for cl in range(2):
                 h[q, 3 + cl, 4:12, :] = own[it, q, cl]
-        for copy in halo:
+        for copy in halo[4:]:
             copy.wait_recv()
         for q in range(4):
             h[q, 0, 4:12, :] = left2[it, q]
             h[q, 7, 4:12, :] = right2[it, q]
             for cl in range(2):
                 h[q, 1 + cl, 4:12, :] = left1[it, q, cl]
+                h[q, 5 + cl, 4:12, :] = right1[it, q, cl]
+                h[q, 3 + cl, 0:4, :] = north[it, q, cl]
+                h[q, 3 + cl, 12:16, :] = south[it, q, cl]
+
+        def first_guess(j, carry):
+            guess_on(j, 0, 8)
+            guess_on(j, 8, 8)
+            return carry
+
+        lax.fori_loop(0, 8, first_guess, 0, unroll=2)
+        for copy in halo[:4]:
+            copy.wait_recv()
+        for cl in range(2):
+            for q in range(4):
                 h[q, 1 + cl, 2:4, :] = nw[it, q, cl]
                 h[q, 1 + cl, 12:14, :] = sw[it, q, cl]
-                h[q, 5 + cl, 4:12, :] = right1[it, q, cl]
                 h[q, 5 + cl, 2:4, :] = ne[it, q, cl]
                 h[q, 5 + cl, 12:14, :] = se[it, q, cl]
-                h[q, 3 + cl, 0:4, :] = north[it, q, cl]
-                h[q, 3 + cl, 12:16, :] = south[it, q, cl]
-
-        def first_guess(j, carry):
-            for at in (0, 8):
-                rows = pl.ds(at, 8)
-                for q in range(2):
-                    re, im = h[q, j, rows, :], h[q + 2, j, rows, :]
-                    p_re, p_im, p_x = lead[0, q, j, rows, :], lead[1, q, j, rows, :], lead[2, q, j, rows, :]
-                    wa[q, j, pl.ds(8 + at, 8), :] = p_re * re + p_x * im
-                    wa[q + 2, j, pl.ds(8 + at, 8), :] = p_im * im - p_x * re
-            return carry
-
-        lax.fori_loop(0, 8, first_guess, 0)
+            for j in (1 + cl, 5 + cl):
+                for first in (2, 12):
+                    guess_on(j, first, 2)
         sweep(wa, wb, 1, 7)
         sweep(wb, wa, 2, 6)
         guess, image = [], []
         for cl in range(2):
             j = 3 + cl
             w_row, g_row = [None] * 4, [None] * 4
+            weights = weights_of(j, 4)
             for q in range(2):
-                s_re, s_im, s_x = shifts(q)
-                w_re, b_re = stencil(wa, q, j, 12, 8, 4)
-                w_im, b_im = stencil(wa, q + 2, j, 12, 8, 4)
+                s_re, s_im, s_x = shifts[q]
+                w_re, b_re = stencil(wa, q, j, 12, weights)
+                w_im, b_im = stencil(wa, q + 2, j, 12, weights)
                 w_row[q], w_row[q + 2] = w_re, w_im
                 g_row[q] = b_re - (s_re * w_re + s_x * w_im)
                 g_row[q + 2] = b_im - (s_im * w_im - s_x * w_re)
@@ -549,7 +569,8 @@
         )
         directions.append(both[0:16])
         vectors.append(both[16:32])
-        send_strip(it)
+        if it + 1 < KRYLOV:
+            send_strip(it)
         for i in range(it + 2):
             grams[i, it + 1] = dot_pairs(vectors[i], vectors[it + 1])
         if it == 1:
@@ -595,6 +616,7 @@
         (d * 4 + c, place(((z + d) % 8) * 16 + e_me, (x + c) % 4)) for d, c in FAR_32
     ]
     adds = add_start(mine, ars1, ar1, a1_s, a1_r, others, z * 4 + x)
+    send_strip(2)
     send_steps(1)
     mine = add_end(adds, ar1)
     adds = add_start(mine, ars0, ar0, a0_s, a0_r, [(d, place(z * 16 + (e_me + d) % 16, x)) for d in FAR_16], e_me)
@@ -624,14 +646,14 @@
         for it in range(KRYLOV):
             total = total + on_vectors[it + 1] * r4[it, zz, 1]
         sums[1].append(total)
-    for f, out in ((0, sol_ref), (1, res_ref)):
+    for f in range(2):
         for t in range(4):
             for hh in range(2):
                 value = None
                 for k in range(4):
                     piece = turn(sums[f][hh * 4 + k], k * 32 - t * 32)
                     value = piece if value is None else jnp.where(lane_block(k), piece, value)
-                out[t, :, hh * 128 : hh * 128 + 128] = value
+                out_ref[f, t, :, hh * 128 : hh * 128 + 128] = value
     for copy in started:
         copy.wait_send()
 
@@ -647,12 +669,11 @@
     def sems(*shape):
         return pltpu.SemaphoreType.DMA(shape)
 
-    out = jax.ShapeDtypeStruct(right_side.shape, F32)
-    return pl.pallas_call(
+    both = pl.pallas_call(
         kernel,
-        out_shape=(out, out),
+        out_shape=jax.ShapeDtypeStruct((2, *right_side.shape), F32),
         in_specs=[hbm] * 6,
-        out_specs=(vmem, vmem),
+        out_specs=vmem,
         scratch_shapes=[
             buffer(4, 8, 256), buffer(8, 256), buffer(2, 8, 256), buffer(16, 128), buffer(L, L), buffer(L, L),
             buffer(8, 8, 128), buffer(8, 8, 128), buffer(128, 128), buffer(16, 4, 128), buffer(16, 4, 128),
@@ -675,6 +696,7 @@
             collective_id=0, has_side_effects=True, vmem_limit_bytes=40_000_000
         ),
     )(*[pltpu.with_memory_space_constraint(v, pltpu.HBM) for v in (right_side, diffusion, velocity, jnp.asarray(small), jnp.asarray(forward), jnp.asarray(inverse))])
+    return both[0], both[1]
 
 
 def solution(mesh):

time: 56.2 us -> 55.6 us (0.989)
  local copies, waits for them, and re-layouts: 1.23 us -> 0.63 us
    unnamed x2 -> x0, local copies, waits for them, and re-layouts: 1.23 us -> none
    squeeze x0 -> x1, local copies, waits for them, and re-layouts: none -> 0.63 us  [per_device(): return (both[0], both[1])]
where the time goes in v4:
time: 55.6 us; the launch traced here: 55.5 us
  Pallas kernels  54.2 us (97%)
  between operations  0.64 us (1%)
  local copies, waits for them, and re-layouts  0.63 us (1%)
    pallas_call x1, Pallas kernels, per_device(): pl.pallas_call(kernel, out_shape=jax.ShapeDtypeStruct((2, *right_side.sha...  54.2 us

profile of v4, /device:TPU:1, one launch (start us, length us, event | category | flops | bytes accessed | tf_op | source)
XLA Modules:
  0.0 55.5 jit_solution(13926624538420806969)
XLA Ops:
  0.6 54.2 %shard_map.77 = f32[2,4,8,256]{3,2,1,0:T(8,128)S(1)} custom-call(f32[4,8,256]{2,1,0:T(8,128)} %b_hbm.1, f32[8,256]{1,0:T(8,128)} %diff_hbm.1, f32[2,8,256]{2,1,0:T(8,128)} %vel_hbm.1, f32[16,128]{1,0:T(8,128)} %constant.6.clone.small_hbm, f32[512,512]{1,0:T(8,128)} %constant.7.clone.fwd_hbm, f32[512,512]{1,0:T(8,128)} %constant.8.clone.inv_hbm), custom_call_target="tpu_custom_call" | custom-call | tf_op jit(solution)/shard_map/pallas_call | solution.py:672
  54.8 0.6 %slice_bitcast_fusion = (f32[4,8,256]{2,1,0:T(8,128)}, f32[4,8,256]{2,1,0:T(8,128)}) fusion(f32[2,4,8,256]{3,2,1,0:T(8,128)S(1)} %shard_map.77), kind=kLoop, calls=%fused_computation | loop fusion | bytes 131072 | tf_op jit(solution)/shard_map/squeeze | solution.py:699

commit v5 on v4

--- a/solution.py
+++ b/solution.py
@@ -257,6 +257,10 @@
 
     started = []
 
+    def drain(keep):
+        while len(started) > keep:
+            started.pop(0).wait_send()
+
     def send(src, dst, s_sem, r_sem, device):
         copy = pltpu.make_async_remote_copy(
             src_ref=src, dst_ref=dst, send_sem=s_sem, recv_sem=r_sem, device_id=device, device_id_type=MESH
@@ -621,6 +625,7 @@
     mine = add_end(adds, ar1)
     adds = add_start(mine, ars0, ar0, a0_s, a0_r, [(d, place(z * 16 + (e_me + d) % 16, x)) for d in FAR_16], e_me)
     send_steps(2)
+    drain(len(FAR_16) + len(FAR_8))
     mine = add_end(adds, ar0)
     mine = jnp.broadcast_to(mine, (8, 128))
     gram = [[None] * (KRYLOV + 1) for _ in range(KRYLOV + 1)]
@@ -654,8 +659,7 @@
                     piece = turn(sums[f][hh * 4 + k], k * 32 - t * 32)
                     value = piece if value is None else jnp.where(lane_block(k), piece, value)
                 out_ref[f, t, :, hh * 128 : hh * 128 + 128] = value
-    for copy in started:
-        copy.wait_send()
+    drain(0)
 
 
 def per_device(right_side, diffusion, velocity):

time: 55.6 us -> 55.4 us (level)
  no operation moved by 1% of the time
where the time goes in v5:
time: 55.4 us; the launch traced here: 55.2 us
  Pallas kernels  54 us (97%)
  between operations  0.64 us (1%)
  local copies, waits for them, and re-layouts  0.63 us (1%)
    pallas_call x1, Pallas kernels, per_device(): pl.pallas_call(kernel, out_shape=jax.ShapeDtypeStruct((2, *right_side.sha...  54 us

profile of v5, /device:TPU:1, one launch (start us, length us, event | category | flops | bytes accessed | tf_op | source)
XLA Modules:
  0.0 55.2 jit_solution(16596518673614261187)
XLA Ops:
  0.6 54.0 %shard_map.77 = f32[2,4,8,256]{3,2,1,0:T(8,128)S(1)} custom-call(f32[4,8,256]{2,1,0:T(8,128)} %b_hbm.1, f32[8,256]{1,0:T(8,128)} %diff_hbm.1, f32[2,8,256]{2,1,0:T(8,128)} %vel_hbm.1, f32[16,128]{1,0:T(8,128)} %constant.6.clone.small_hbm, f32[512,512]{1,0:T(8,128)} %constant.7.clone.fwd_hbm, f32[512,512]{1,0:T(8,128)} %constant.8.clone.inv_hbm), custom_call_target="tpu_custom_call" | custom-call | tf_op jit(solution)/shard_map/pallas_call | solution.py:676
  54.6 0.6 %slice_bitcast_fusion = (f32[4,8,256]{2,1,0:T(8,128)}, f32[4,8,256]{2,1,0:T(8,128)}) fusion(f32[2,4,8,256]{3,2,1,0:T(8,128)S(1)} %shard_map.77), kind=kLoop, calls=%fused_computation | loop fusion | bytes 131072 | tf_op jit(solution)/shard_map/squeeze | solution.py:703
